TPU v7x, 32 devices: a 4x4x1 block of a 4x4x8 slice. The times are simulated.
32 devices in a mesh: dp: 1 (over z), tp: 4 (over y), pp: 8 (over x, core).
Axes of the slice: x: 4, y: 4, z: 1, core: 2. Of those that a mesh axis runs over, the one named last changes fastest.
The devices are a block of a 4x4x8 slice.
Arguments:
- x_micro: bfloat16 [8, 6, 128, 1536], P(None, 'dp')
- ln1_gain: bfloat16 [8, 1536], P('pp')
- ln1_bias: bfloat16 [8, 1536], P('pp')
- w_qkv: bfloat16 [8, 3, 1536, 16, 96], P('pp', None, None, 'tp')
- b_qkv: bfloat16 [8, 3, 16, 96], P('pp', None, 'tp')
- w_out: bfloat16 [8, 16, 96, 1536], P('pp', 'tp')
- b_out: bfloat16 [8, 1536], P('pp')
- ln2_gain: bfloat16 [8, 1536], P('pp')
- ln2_bias: bfloat16 [8, 1536], P('pp')
- w_up: bfloat16 [8, 1536, 6144], P('pp', None, 'tp')
- b_up: bfloat16 [8, 6144], P('pp', 'tp')
- w_down: bfloat16 [8, 6144, 1536], P('pp', 'tp')
- b_down: bfloat16 [8, 1536], P('pp')
Outputs:
- output: bfloat16 [8, 8, 6, 128, 1536], P('pp', None, 'dp')
All inputs are finite; a program needn't handle non-finite values.
Results may differ from a plain program's by a relative error of at most 0.02.
Values are sent between devices in bfloat16 or wider.
A program may use at most 768 MiB of HBM per device.

v0:
```python
import jax
import jax.numpy as jnp
from jax import lax
from jax.sharding import PartitionSpec as P

LN_EPS = 1e-5


def layer_norm(act_in, gain_vec, bias_vec):
    act_f32 = act_in.astype(jnp.float32)
    row_mean = jnp.mean(act_f32, axis=-1, keepdims=True)
    centered = act_f32 - row_mean
    row_var = jnp.mean(centered * centered, axis=-1, keepdims=True)
    normed = centered * lax.rsqrt(row_var + LN_EPS)
    return (normed * gain_vec.astype(jnp.float32) + bias_vec.astype(jnp.float32)).astype(jnp.bfloat16)


def stage_layer(act_in, layer_params):
    ln1_gain, ln1_bias, w_qkv, b_qkv, w_out, b_out, ln2_gain, ln2_bias, w_up, b_up, w_down, b_down = layer_params
    head_dim = w_qkv.shape[-1]
    seq_len = act_in.shape[1]
    normed_in = layer_norm(act_in, ln1_gain, ln1_bias)
    qkv_proj = (jnp.einsum('bsd,cdhe->cbshe', normed_in, w_qkv, preferred_element_type=jnp.float32) + b_qkv[:, None, None].astype(jnp.float32)).astype(jnp.bfloat16)
    scores = jnp.einsum('bqhe,bkhe->bhqk', qkv_proj[0], qkv_proj[1], preferred_element_type=jnp.float32) * (head_dim ** -0.5)
    causal = lax.broadcasted_iota(jnp.int32, (seq_len, seq_len), 0) >= lax.broadcasted_iota(jnp.int32, (seq_len, seq_len), 1)
    attn_probs = jax.nn.softmax(jnp.where(causal, scores, -1e30), axis=-1).astype(jnp.bfloat16)
    context = jnp.einsum('bhqk,bkhe->bqhe', attn_probs, qkv_proj[2], preferred_element_type=jnp.float32).astype(jnp.bfloat16)
    attn_part = jnp.einsum('crif,ife->cre', context, w_out, preferred_element_type=jnp.float32).astype(jnp.bfloat16)
    attn_out = (lax.psum(attn_part, 'tp').astype(jnp.float32) + b_out.astype(jnp.float32)).astype(jnp.bfloat16)
    resid_mid = (act_in.astype(jnp.float32) + attn_out.astype(jnp.float32)).astype(jnp.bfloat16)
    normed_mid = layer_norm(resid_mid, ln2_gain, ln2_bias)
    hidden_up = jax.nn.gelu(jnp.einsum('bsd,df->bsf', normed_mid, w_up, preferred_element_type=jnp.float32) + b_up.astype(jnp.float32), approximate=True).astype(jnp.bfloat16)
    mlp_part = jnp.einsum('bsf,fd->bsd', hidden_up, w_down, preferred_element_type=jnp.float32).astype(jnp.bfloat16)
    mlp_out = (lax.psum(mlp_part, 'tp').astype(jnp.float32) + b_down.astype(jnp.float32)).astype(jnp.bfloat16)
    return (resid_mid.astype(jnp.float32) + mlp_out.astype(jnp.float32)).astype(jnp.bfloat16)


def solution(mesh):
    stages = mesh.shape['pp']
    shift_pairs = [(source_idx, source_idx + 1) for source_idx in range(stages - 1)]
    weight_specs = (
        P('pp', None), P('pp', None),
        P('pp', None, None, 'tp', None), P('pp', None, 'tp', None),
        P('pp', 'tp', None, None), P('pp', None),
        P('pp', None), P('pp', None),
        P('pp', None, 'tp'), P('pp', 'tp'),
        P('pp', 'tp', None), P('pp', None),
    )

    def local_run(x_micro, ln1_gain, ln1_bias, w_qkv, b_qkv, w_out, b_out, ln2_gain, ln2_bias, w_up, b_up, w_down, b_down):
        layer_params = tuple(stacked[0] for stacked in (ln1_gain, ln1_bias, w_qkv, b_qkv, w_out, b_out, ln2_gain, ln2_bias, w_up, b_up, w_down, b_down))
        micro_count = x_micro.shape[0]
        stage_idx = lax.axis_index('pp')

        def time_step(tick, loop_state):
            received, out_buf = loop_state
            first_in = lax.dynamic_index_in_dim(x_micro, jnp.minimum(tick, micro_count - 1), 0, keepdims=False)
            stage_in = jnp.where(stage_idx == 0, first_in, received)
            stage_out = stage_layer(stage_in, layer_params)
            micro_idx = tick - stage_idx
            is_valid = (micro_idx >= 0) & (micro_idx < micro_count)
            slot_idx = jnp.clip(micro_idx, 0, micro_count - 1)
            old_slot = lax.dynamic_index_in_dim(out_buf, slot_idx, 0, keepdims=False)
            out_buf = lax.dynamic_update_index_in_dim(out_buf, jnp.where(is_valid, stage_out, old_slot), slot_idx, 0)
            received = lax.ppermute(stage_out, 'pp', shift_pairs)
            return received, out_buf

        start_state = (jnp.zeros(x_micro.shape[1:], jnp.bfloat16), jnp.zeros(x_micro.shape, jnp.bfloat16))
        final_recv, out_buf = lax.fori_loop(0, micro_count + stages - 1, time_step, start_state)
        return out_buf[None]

    return jax.shard_map(local_run, mesh=mesh, in_specs=(P(None, 'dp', None, None),) + weight_specs, out_specs=P('pp', None, 'dp', None, None), check_vma=False)
```

profile of v0, /device:TPU:103, one launch (start us, length us, event | category | flops | bytes accessed | tf_op | source)
XLA Modules:
  0.0 2813.8 jit_solution(10299344624684550348)
XLA Ops:
  19.9 2787.1 %while.16 = (s32[]{:T(128)}, bf16[6,128,1536]{2,1,0:T(8,128)(2,1)}, bf16[8,6,128,1536]{3,2,1,0:T(8,128)(2,1)}, pred[]{:T(512)}, bf16[8,6,128,1536]{3,2,1,0:T(8,1...) while((s32[]{:T(128)}, bf16[6,128,1536]{2,1,0:T(8,128)(2,1)}, ...), condition=%wide.region_9.10_spmd, body=%wide.region_0.9_spmd.sunk | while | flops 11090785280 | bytes 164989792 | solution.py:69
  37.6 60.1 %all-reduce.3.cloned.1.call-done = bf16[6,128,1536]{2,1,0:T(8,128)(2,1)} async-done(((bf16[6,128,1536]{2,1,0:T(8,128)(2,1)}), bf16[6,128,1536]{2,1,0:T(8,128)(2,1)}) %all-reduce.3.cloned.1.call-update) | async-done | bytes 2359312 | tf_op jit(solution)/shard_map/while/body/eval_jaxpr/psum | solution.py:29
  118.4 54.1 %all-reduce.5.cloned.1.call-done = bf16[6,128,1536]{2,1,0:T(8,128)(2,1)} async-done(((bf16[6,128,1536]{2,1,0:T(8,128)(2,1)}), bf16[6,128,1536]{2,1,0:T(8,128)(2,1)}) %all-reduce.5.cloned.1.call-update) | async-done | bytes 2359312 | tf_op jit(solution)/shard_map/while/body/eval_jaxpr/psum | solution.py:34
  204.1 80.8 %all-reduce.3.cloned.1.call-done = bf16[6,128,1536]{2,1,0:T(8,128)(2,1)} async-done(((bf16[6,128,1536]{2,1,0:T(8,128)(2,1)}), bf16[6,128,1536]{2,1,0:T(8,128)(2,1)}) %all-reduce.3.cloned.1.call-update) | async-done | bytes 2359312 | tf_op jit(solution)/shard_map/while/body/eval_jaxpr/psum | solution.py:29
  305.6 54.0 %all-reduce.5.cloned.1.call-done = bf16[6,128,1536]{2,1,0:T(8,128)(2,1)} async-done(((bf16[6,128,1536]{2,1,0:T(8,128)(2,1)}), bf16[6,128,1536]{2,1,0:T(8,128)(2,1)}) %all-reduce.5.cloned.1.call-update) | async-done | bytes 2359312 | tf_op jit(solution)/shard_map/while/body/eval_jaxpr/psum | solution.py:34
  391.3 80.8 %all-reduce.3.cloned.1.call-done = bf16[6,128,1536]{2,1,0:T(8,128)(2,1)} async-done(((bf16[6,128,1536]{2,1,0:T(8,128)(2,1)}), bf16[6,128,1536]{2,1,0:T(8,128)(2,1)}) %all-reduce.3.cloned.1.call-update) | async-done | bytes 2359312 | tf_op jit(solution)/shard_map/while/body/eval_jaxpr/psum | solution.py:29
  492.8 54.0 %all-reduce.5.cloned.1.call-done = bf16[6,128,1536]{2,1,0:T(8,128)(2,1)} async-done(((bf16[6,128,1536]{2,1,0:T(8,128)(2,1)}), bf16[6,128,1536]{2,1,0:T(8,128)(2,1)}) %all-reduce.5.cloned.1.call-update) | async-done | bytes 2359312 | tf_op jit(solution)/shard_map/while/body/eval_jaxpr/psum | solution.py:34
  578.5 80.8 %all-reduce.3.cloned.1.call-done = bf16[6,128,1536]{2,1,0:T(8,128)(2,1)} async-done(((bf16[6,128,1536]{2,1,0:T(8,128)(2,1)}), bf16[6,128,1536]{2,1,0:T(8,128)(2,1)}) %all-reduce.3.cloned.1.call-update) | async-done | bytes 2359312 | tf_op jit(solution)/shard_map/while/body/eval_jaxpr/psum | solution.py:29
  680.0 54.0 %all-reduce.5.cloned.1.call-done = bf16[6,128,1536]{2,1,0:T(8,128)(2,1)} async-done(((bf16[6,128,1536]{2,1,0:T(8,128)(2,1)}), bf16[6,128,1536]{2,1,0:T(8,128)(2,1)}) %all-reduce.5.cloned.1.call-update) | async-done | bytes 2359312 | tf_op jit(solution)/shard_map/while/body/eval_jaxpr/psum | solution.py:34
  765.7 80.8 %all-reduce.3.cloned.1.call-done = bf16[6,128,1536]{2,1,0:T(8,128)(2,1)} async-done(((bf16[6,128,1536]{2,1,0:T(8,128)(2,1)}), bf16[6,128,1536]{2,1,0:T(8,128)(2,1)}) %all-reduce.3.cloned.1.call-update) | async-done | bytes 2359312 | tf_op jit(solution)/shard_map/while/body/eval_jaxpr/psum | solution.py:29
  952.8 80.8 %all-reduce.3.cloned.1.call-done = bf16[6,128,1536]{2,1,0:T(8,128)(2,1)} async-done(((bf16[6,128,1536]{2,1,0:T(8,128)(2,1)}), bf16[6,128,1536]{2,1,0:T(8,128)(2,1)}) %all-reduce.3.cloned.1.call-update) | async-done | bytes 2359312 | tf_op jit(solution)/shard_map/while/body/eval_jaxpr/psum | solution.py:29
  1054.3 54.0 %all-reduce.5.cloned.1.call-done = bf16[6,128,1536]{2,1,0:T(8,128)(2,1)} async-done(((bf16[6,128,1536]{2,1,0:T(8,128)(2,1)}), bf16[6,128,1536]{2,1,0:T(8,128)(2,1)}) %all-reduce.5.cloned.1.call-update) | async-done | bytes 2359312 | tf_op jit(solution)/shard_map/while/body/eval_jaxpr/psum | solution.py:34
  1140.0 80.8 %all-reduce.3.cloned.1.call-done = bf16[6,128,1536]{2,1,0:T(8,128)(2,1)} async-done(((bf16[6,128,1536]{2,1,0:T(8,128)(2,1)}), bf16[6,128,1536]{2,1,0:T(8,128)(2,1)}) %all-reduce.3.cloned.1.call-update) | async-done | bytes 2359312 | tf_op jit(solution)/shard_map/while/body/eval_jaxpr/psum | solution.py:29
  1241.5 54.0 %all-reduce.5.cloned.1.call-done = bf16[6,128,1536]{2,1,0:T(8,128)(2,1)} async-done(((bf16[6,128,1536]{2,1,0:T(8,128)(2,1)}), bf16[6,128,1536]{2,1,0:T(8,128)(2,1)}) %all-reduce.5.cloned.1.call-update) | async-done | bytes 2359312 | tf_op jit(solution)/shard_map/while/body/eval_jaxpr/psum | solution.py:34
  1327.2 80.8 %all-reduce.3.cloned.1.call-done = bf16[6,128,1536]{2,1,0:T(8,128)(2,1)} async-done(((bf16[6,128,1536]{2,1,0:T(8,128)(2,1)}), bf16[6,128,1536]{2,1,0:T(8,128)(2,1)}) %all-reduce.3.cloned.1.call-update) | async-done | bytes 2359312 | tf_op jit(solution)/shard_map/while/body/eval_jaxpr/psum | solution.py:29
  1428.7 54.0 %all-reduce.5.cloned.1.call-done = bf16[6,128,1536]{2,1,0:T(8,128)(2,1)} async-done(((bf16[6,128,1536]{2,1,0:T(8,128)(2,1)}), bf16[6,128,1536]{2,1,0:T(8,128)(2,1)}) %all-reduce.5.cloned.1.call-update) | async-done | bytes 2359312 | tf_op jit(solution)/shard_map/while/body/eval_jaxpr/psum | solution.py:34
  1514.4 80.8 %all-reduce.3.cloned.1.call-done = bf16[6,128,1536]{2,1,0:T(8,128)(2,1)} async-done(((bf16[6,128,1536]{2,1,0:T(8,128)(2,1)}), bf16[6,128,1536]{2,1,0:T(8,128)(2,1)}) %all-reduce.3.cloned.1.call-update) | async-done | bytes 2359312 | tf_op jit(solution)/shard_map/while/body/eval_jaxpr/psum | solution.py:29
  1615.9 54.0 %all-reduce.5.cloned.1.call-done = bf16[6,128,1536]{2,1,0:T(8,128)(2,1)} async-done(((bf16[6,128,1536]{2,1,0:T(8,128)(2,1)}), bf16[6,128,1536]{2,1,0:T(8,128)(2,1)}) %all-reduce.5.cloned.1.call-update) | async-done | bytes 2359312 | tf_op jit(solution)/shard_map/while/body/eval_jaxpr/psum | solution.py:34
  1701.6 80.8 %all-reduce.3.cloned.1.call-done = bf16[6,128,1536]{2,1,0:T(8,128)(2,1)} async-done(((bf16[6,128,1536]{2,1,0:T(8,128)(2,1)}), bf16[6,128,1536]{2,1,0:T(8,128)(2,1)}) %all-reduce.3.cloned.1.call-update) | async-done | bytes 2359312 | tf_op jit(solution)/shard_map/while/body/eval_jaxpr/psum | solution.py:29
  1888.8 80.8 %all-reduce.3.cloned.1.call-done = bf16[6,128,1536]{2,1,0:T(8,128)(2,1)} async-done(((bf16[6,128,1536]{2,1,0:T(8,128)(2,1)}), bf16[6,128,1536]{2,1,0:T(8,128)(2,1)}) %all-reduce.3.cloned.1.call-update) | async-done | bytes 2359312 | tf_op jit(solution)/shard_map/while/body/eval_jaxpr/psum | solution.py:29
  2075.9 80.8 %all-reduce.3.cloned.1.call-done = bf16[6,128,1536]{2,1,0:T(8,128)(2,1)} async-done(((bf16[6,128,1536]{2,1,0:T(8,128)(2,1)}), bf16[6,128,1536]{2,1,0:T(8,128)(2,1)}) %all-reduce.3.cloned.1.call-update) | async-done | bytes 2359312 | tf_op jit(solution)/shard_map/while/body/eval_jaxpr/psum | solution.py:29
  2263.1 80.8 %all-reduce.3.cloned.1.call-done = bf16[6,128,1536]{2,1,0:T(8,128)(2,1)} async-done(((bf16[6,128,1536]{2,1,0:T(8,128)(2,1)}), bf16[6,128,1536]{2,1,0:T(8,128)(2,1)}) %all-reduce.3.cloned.1.call-update) | async-done | bytes 2359312 | tf_op jit(solution)/shard_map/while/body/eval_jaxpr/psum | solution.py:29
  2450.3 80.8 %all-reduce.3.cloned.1.call-done = bf16[6,128,1536]{2,1,0:T(8,128)(2,1)} async-done(((bf16[6,128,1536]{2,1,0:T(8,128)(2,1)}), bf16[6,128,1536]{2,1,0:T(8,128)(2,1)}) %all-reduce.3.cloned.1.call-update) | async-done | bytes 2359312 | tf_op jit(solution)/shard_map/while/body/eval_jaxpr/psum | solution.py:29
  2637.5 80.8 %all-reduce.3.cloned.1.call-done = bf16[6,128,1536]{2,1,0:T(8,128)(2,1)} async-done(((bf16[6,128,1536]{2,1,0:T(8,128)(2,1)}), bf16[6,128,1536]{2,1,0:T(8,128)(2,1)}) %all-reduce.3.cloned.1.call-update) | async-done | bytes 2359312 | tf_op jit(solution)/shard_map/while/body/eval_jaxpr/psum | solution.py:29
  (663 shorter events, 1173.0 us)
Async XLA Ops:
  37.5 135.0 %all-reduce.5.cloned.1.call-start = ((), (), s32[]{:S(2)}) async-start(), calls=%async_computation.1 | async-start | bytes 4718592 | tf_op jit(solution)/shard_map/while/body/eval_jaxpr/psum | solution.py:34
  204.0 155.7 %all-reduce.5.cloned.1.call-start = ((), (), s32[]{:S(2)}) async-start(), calls=%async_computation.1 | async-start | bytes 4718592 | tf_op jit(solution)/shard_map/while/body/eval_jaxpr/psum | solution.py:34
  391.2 155.7 %all-reduce.5.cloned.1.call-start = ((), (), s32[]{:S(2)}) async-start(), calls=%async_computation.1 | async-start | bytes 4718592 | tf_op jit(solution)/shard_map/while/body/eval_jaxpr/psum | solution.py:34
  560.8 98.5 %all-reduce.3.cloned.1.call-start = ((), (), s32[]{:S(2)}) async-start(), calls=%async_computation | async-start | bytes 4718592 | tf_op jit(solution)/shard_map/while/body/eval_jaxpr/psum | solution.py:29
  578.4 155.7 %all-reduce.5.cloned.1.call-start = ((), (), s32[]{:S(2)}) async-start(), calls=%async_computation.1 | async-start | bytes 4718592 | tf_op jit(solution)/shard_map/while/body/eval_jaxpr/psum | solution.py:34
  747.9 98.5 %all-reduce.3.cloned.1.call-start = ((), (), s32[]{:S(2)}) async-start(), calls=%async_computation | async-start | bytes 4718592 | tf_op jit(solution)/shard_map/while/body/eval_jaxpr/psum | solution.py:29
  765.5 155.7 %all-reduce.5.cloned.1.call-start = ((), (), s32[]{:S(2)}) async-start(), calls=%async_computation.1 | async-start | bytes 4718592 | tf_op jit(solution)/shard_map/while/body/eval_jaxpr/psum | solution.py:34
  935.1 98.5 %all-reduce.3.cloned.1.call-start = ((), (), s32[]{:S(2)}) async-start(), calls=%async_computation | async-start | bytes 4718592 | tf_op jit(solution)/shard_map/while/body/eval_jaxpr/psum | solution.py:29
  952.7 155.7 %all-reduce.5.cloned.1.call-start = ((), (), s32[]{:S(2)}) async-start(), calls=%async_computation.1 | async-start | bytes 4718592 | tf_op jit(solution)/shard_map/while/body/eval_jaxpr/psum | solution.py:34
  1122.3 98.5 %all-reduce.3.cloned.1.call-start = ((), (), s32[]{:S(2)}) async-start(), calls=%async_computation | async-start | bytes 4718592 | tf_op jit(solution)/shard_map/while/body/eval_jaxpr/psum | solution.py:29
  1139.9 155.7 %all-reduce.5.cloned.1.call-start = ((), (), s32[]{:S(2)}) async-start(), calls=%async_computation.1 | async-start | bytes 4718592 | tf_op jit(solution)/shard_map/while/body/eval_jaxpr/psum | solution.py:34
  1309.5 98.5 %all-reduce.3.cloned.1.call-start = ((), (), s32[]{:S(2)}) async-start(), calls=%async_computation | async-start | bytes 4718592 | tf_op jit(solution)/shard_map/while/body/eval_jaxpr/psum | solution.py:29
  1327.1 155.7 %all-reduce.5.cloned.1.call-start = ((), (), s32[]{:S(2)}) async-start(), calls=%async_computation.1 | async-start | bytes 4718592 | tf_op jit(solution)/shard_map/while/body/eval_jaxpr/psum | solution.py:34
  1496.7 98.5 %all-reduce.3.cloned.1.call-start = ((), (), s32[]{:S(2)}) async-start(), calls=%async_computation | async-start | bytes 4718592 | tf_op jit(solution)/shard_map/while/body/eval_jaxpr/psum | solution.py:29
  1514.3 155.7 %all-reduce.5.cloned.1.call-start = ((), (), s32[]{:S(2)}) async-start(), calls=%async_computation.1 | async-start | bytes 4718592 | tf_op jit(solution)/shard_map/while/body/eval_jaxpr/psum | solution.py:34
  1701.5 155.7 %all-reduce.5.cloned.1.call-start = ((), (), s32[]{:S(2)}) async-start(), calls=%async_computation.1 | async-start | bytes 4718592 | tf_op jit(solution)/shard_map/while/body/eval_jaxpr/psum | solution.py:34
  1888.6 155.7 %all-reduce.5.cloned.1.call-start = ((), (), s32[]{:S(2)}) async-start(), calls=%async_computation.1 | async-start | bytes 4718592 | tf_op jit(solution)/shard_map/while/body/eval_jaxpr/psum | solution.py:34
  2075.8 155.7 %all-reduce.5.cloned.1.call-start = ((), (), s32[]{:S(2)}) async-start(), calls=%async_computation.1 | async-start | bytes 4718592 | tf_op jit(solution)/shard_map/while/body/eval_jaxpr/psum | solution.py:34
  2245.4 98.5 %all-reduce.3.cloned.1.call-start = ((), (), s32[]{:S(2)}) async-start(), calls=%async_computation | async-start | bytes 4718592 | tf_op jit(solution)/shard_map/while/body/eval_jaxpr/psum | solution.py:29
  2263.0 155.7 %all-reduce.5.cloned.1.call-start = ((), (), s32[]{:S(2)}) async-start(), calls=%async_computation.1 | async-start | bytes 4718592 | tf_op jit(solution)/shard_map/while/body/eval_jaxpr/psum | solution.py:34
  2432.6 98.5 %all-reduce.3.cloned.1.call-start = ((), (), s32[]{:S(2)}) async-start(), calls=%async_computation | async-start | bytes 4718592 | tf_op jit(solution)/shard_map/while/body/eval_jaxpr/psum | solution.py:29
  2450.2 155.7 %all-reduce.5.cloned.1.call-start = ((), (), s32[]{:S(2)}) async-start(), calls=%async_computation.1 | async-start | bytes 4718592 | tf_op jit(solution)/shard_map/while/body/eval_jaxpr/psum | solution.py:34
  2619.8 98.5 %all-reduce.3.cloned.1.call-start = ((), (), s32[]{:S(2)}) async-start(), calls=%async_computation | async-start | bytes 4718592 | tf_op jit(solution)/shard_map/while/body/eval_jaxpr/psum | solution.py:29
  2637.4 155.7 %all-reduce.5.cloned.1.call-start = ((), (), s32[]{:S(2)}) async-start(), calls=%async_computation.1 | async-start | bytes 4718592 | tf_op jit(solution)/shard_map/while/body/eval_jaxpr/psum | solution.py:34
  (112 other events, 2034.8 us)
Sparse Core Ops, SparseCore 0:
  37.6 60.0 all-reduce.2
  115.0 57.4 all-reduce.4
  204.1 80.7 all-reduce.2
  302.2 57.4 all-reduce.4
  391.3 80.7 all-reduce.2
  489.4 57.4 all-reduce.4
  578.5 80.7 all-reduce.2
  676.6 57.4 all-reduce.4
  765.7 80.7 all-reduce.2
  863.7 57.4 all-reduce.4
  952.8 80.7 all-reduce.2
  1050.9 57.4 all-reduce.4
  1140.0 80.7 all-reduce.2
  1238.1 57.4 all-reduce.4
  1327.2 80.7 all-reduce.2
  1425.3 57.4 all-reduce.4
  1514.4 80.7 all-reduce.2
  1612.5 57.4 all-reduce.4
  1701.6 80.7 all-reduce.2
  1888.8 80.7 all-reduce.2
  2075.9 80.7 all-reduce.2
  2263.1 80.7 all-reduce.2
  2450.3 80.7 all-reduce.2
  2637.5 80.7 all-reduce.2
  (6 shorter events, 344.2 us)
where the time goes:
time: 2840 us; the launch traced here: 2810 us
  waiting for transfers between devices  2090 us (74%)
  matrix products  405 us (14%)
  other arithmetic  201 us (7%)
  local copies, waits for them, and re-layouts  82.7 us (3%)
    psum x15, waiting for transfers between devices, stage_layer(): lax.psum(attn_part, 'tp').astype(jnp.float32) + b_out.astype(jnp.float32)  1190 us
    psum x15, waiting for transfers between devices, stage_layer(): lax.psum(mlp_part, 'tp').astype(jnp.float32) + b_down.astype(jnp.float32)  811 us
    dot_general x15, matrix products, stage_layer(): jnp.einsum('bsd,df->bsf', normed_mid, w_up, preferred_element_type=jnp.fl...  127 us
    reduce_sum x30, other arithmetic, layer_norm(): row_mean = jnp.mean(act_f32, axis=-1, keepdims=True)  87.9 us
    dynamic_update_slice x15, other arithmetic, time_step(): lax.dynamic_update_index_in_dim(out_buf, jnp.where(is_valid, stage_out, o...  84.5 us
    ppermute x15, waiting for transfers between devices, time_step(): received = lax.ppermute(stage_out, 'pp', shift_pairs)  83.5 us
    dot_general x15, matrix products, stage_layer(): jnp.einsum('bsd,cdhe->cbshe', normed_in, w_qkv, preferred_element_type=jn...  79.5 us
    dot_general x15, matrix products, stage_layer(): jnp.einsum('bsf,fd->bsd', hidden_up, w_down, preferred_element_type=jnp.f...  77.5 us
  transfers between devices with their start and end apart: 45, of which 45 were waited for; matrix products, arithmetic and copies ran while one was open for 2% of the time, Pallas kernels for 0%

commit v1 on v0

v1 whole, which is shorter than its diff:
```python
import functools

import jax
import jax.numpy as jnp
from jax import lax
from jax.experimental import pallas as pl
from jax.experimental.pallas import tpu as pltpu
from jax.sharding import PartitionSpec as P

LN_EPS = 1e-5
MESH = pl.DeviceIdType.MESH
LN_ROWS = 16
UP_CHUNK = 512
DOWN_CHUNK = 512
OUT_CHUNK = 512
QKV_CHUNK = 768


def _f32(val):
    return val.astype(jnp.float32)


def _norm_rows(rows, gain, bias):
    width = rows.shape[-1]
    mean = jnp.sum(rows, axis=-1, keepdims=True) * (1.0 / width)
    cen = rows - mean
    var = jnp.sum(cen * cen, axis=-1, keepdims=True) * (1.0 / width)
    return (cen * lax.rsqrt(var + LN_EPS) * gain + bias).astype(jnp.bfloat16)


def _dot(lhs, rhs):
    return jnp.dot(lhs, rhs, preferred_element_type=jnp.float32)


def _pipeline_kernel(stages, head_dim, x_hbm, wqkv_hbm, wout_hbm, wup_hbm, wdn_hbm, bqkv_in, bup_in,
                     ln1_gain, ln1_bias, b_out, ln2_gain, ln2_bias, b_down,
                     y_hbm,
                     wqkv, wout, wup, wdn, bqkv, bup, xbuf, hbuf, qkv, obuf, acc, x1buf, ubuf, pown, prcv, ybuf,
                     x_sem, yr_sem, wl_sem, ws_sem, wr_sem, os_sem, or_sem, ps_sem, pr_sem, yl_sem, yn_sem, ye_sem, wb_sem):
    units, seq, d_model = xbuf.shape
    group_w = wout_hbm.shape[0]
    group_heads = group_w // head_dim
    qkv_w = 3 * group_w
    ff = wup_hbm.shape[1]
    rr = lax.axis_index("tp")
    pp = lax.axis_index("pp")
    odd_type = ((pp + 1) // 2) % 2
    even_type = 1 - odd_type
    near, far = rr + 1 - 2 * (rr % 2), 3 - rr
    mate = odd_type * near + even_type * far
    twin = odd_type * far + even_type * near
    cross = rr + 2 - 4 * (rr // 2)
    side = odd_type * (rr % 2) + even_type * (rr // 2)
    twin_side = odd_type * (1 - side) + even_type * side
    half = odd_type * (rr // 2) + even_type * (((rr + 1) // 2) % 2)
    base = half * units
    has_next = pp + 1 < stages
    diag_send = (pp % 2 == 0) & (rr % 2 == 0)
    diag_recv = (pp % 2 == 1) & (rr % 2 == 1)

    def local(src, dst, sem):
        return pltpu.make_async_copy(src, dst, sem)

    def remote(src, dst, send, recv, dev):
        return pltpu.make_async_remote_copy(src_ref=src, dst_ref=dst, send_sem=send, recv_sem=recv, device_id=dev, device_id_type=MESH)

    own_cols, twin_cols = pl.ds(0, qkv_w), pl.ds(qkv_w, qkv_w)
    loads = [
        local(wqkv_hbm, wqkv.at[:, own_cols], wl_sem.at[0]),
        local(bqkv_in, bqkv.at[0], wl_sem.at[1]),
        local(wout_hbm, wout.at[2 * side], wl_sem.at[2]),
        local(wup_hbm, wup.at[0], wl_sem.at[3]),
        local(bup_in, bup.at[0], wl_sem.at[4]),
        local(wdn_hbm, wdn.at[0], wl_sem.at[5]),
    ]
    passes = [
        remote(wqkv_hbm, wqkv.at[:, twin_cols], ws_sem.at[0], wr_sem.at[0], {"tp": twin}),
        remote(bqkv_in, bqkv.at[1], ws_sem.at[1], wr_sem.at[1], {"tp": twin}),
        remote(wout_hbm, wout.at[2 * twin_side + 1], ws_sem.at[2], wr_sem.at[2], {"tp": twin}),
        remote(wout_hbm, wout.at[2 * side], ws_sem.at[3], wr_sem.at[3], {"tp": mate}),
        remote(wout_hbm, wout.at[2 * twin_side + 1], ws_sem.at[4], wr_sem.at[4], {"tp": cross}),
        remote(wup_hbm, wup.at[1], ws_sem.at[5], wr_sem.at[5], {"tp": twin}),
        remote(bup_in, bup.at[1], ws_sem.at[6], wr_sem.at[6], {"tp": twin}),
        remote(wdn_hbm, wdn.at[1], ws_sem.at[7], wr_sem.at[7], {"tp": twin}),
    ]

    def x_copy(k):
        return local(x_hbm.at[base + k], xbuf.at[k], x_sem.at[k])

    loads[0].start()
    loads[1].start()

    @pl.when(pp == 0)
    def _():
        def start_x(k, carry):
            x_copy(k).start()
            return carry
        lax.fori_loop(0, units, start_x, 0)

    for copy in loads[2:]:
        copy.start()

    barrier = pltpu.get_barrier_semaphore()

    def greet(dev):
        pl.semaphore_signal(barrier, inc=1, device_id=dev, device_id_type=MESH)

    for other in (mate, twin, cross):
        greet({"tp": other})

    @pl.when(has_next)
    def _():
        greet({"pp": pp + 1})

    @pl.when(pp > 0)
    def _():
        greet({"pp": pp - 1})

    @pl.when(diag_send)
    def _():
        greet({"tp": twin, "pp": pp + 1})

    @pl.when(diag_recv)
    def _():
        greet({"tp": mate, "pp": pp - 1})

    diag_count = (1 - (pp % 2)) * (1 - (rr % 2)) + (pp % 2) * (rr % 2)
    inner = jnp.where(has_next, 1, 0) + jnp.where(pp > 0, 1, 0)
    pl.semaphore_wait(barrier, 3 + inner + diag_count)

    for copy in passes:
        copy.start()

    def wait_weights(load_idx, pass_idx):
        for idx in load_idx:
            loads[idx].wait()
        for idx in pass_idx:
            passes[idx].wait_recv()

    row_id = lax.broadcasted_iota(jnp.int32, (seq, seq), 0)
    col_id = lax.broadcasted_iota(jnp.int32, (seq, seq), 1)

    def o_copy(slot, grp):
        ref = obuf.at[slot, side, :, pl.ds(grp * group_w, group_w)]
        return remote(ref, ref, os_sem.at[slot, grp], or_sem.at[slot, grp], {"tp": mate})

    def p_copy(slot, idx):
        cols = pl.ds(idx * DOWN_CHUNK, DOWN_CHUNK)
        return remote(pown.at[slot, :, cols], prcv.at[slot, :, cols], ps_sem.at[slot, idx], pr_sem.at[slot, idx], {"tp": mate})

    p_chunks = d_model // DOWN_CHUNK

    def y_local(k, slot):
        return local(ybuf.at[slot], y_hbm.at[base + k], yl_sem.at[slot])

    def y_next(k, slot):
        return remote(ybuf.at[slot], xbuf.at[k], yn_sem.at[slot], x_sem.at[k], {"pp": pp + 1})

    def y_twin(k, slot):
        return remote(ybuf.at[slot], y_hbm.at[base + k], ye_sem.at[slot], yr_sem.at[k], {"tp": twin})

    def y_diag(k, slot):
        return remote(ybuf.at[slot], xbuf.at[k], ye_sem.at[slot], x_sem.at[k], {"tp": twin, "pp": pp + 1})

    sends_next = has_next & ((pp % 2 == 1) | (rr % 2 == 0))

    def y_start(k, slot):
        y_local(k, slot).start()

        @pl.when(sends_next)
        def _():
            y_next(k, slot).start()

        @pl.when(diag_send)
        def _():
            y_diag(k, slot).start()

        @pl.when(jnp.logical_not(diag_send))
        def _():
            y_twin(k, slot).start()

    def y_wait(k, slot):
        y_local(k, slot).wait()

        @pl.when(sends_next)
        def _():
            y_next(k, slot).wait_send()

        @pl.when(diag_send)
        def _():
            y_diag(k, slot).wait_send()

        @pl.when(jnp.logical_not(diag_send))
        def _():
            y_twin(k, slot).wait_send()

    def wb_copy(k, slot):
        return remote(xbuf.at[k], y_hbm.at[base + k], wb_sem.at[slot], yr_sem.at[k], {"pp": pp - 1})

    def attention(k):
        slot = k % 2
        x_copy(k).wait()

        @pl.when(diag_recv)
        def _():
            @pl.when(k >= 2)
            def _():
                wb_copy(k - 2, slot).wait_send()
            wb_copy(k, slot).start()

        gain, bias = _f32(ln1_gain[...]), _f32(ln1_bias[...])
        for r0 in range(0, seq, LN_ROWS):
            rows = pl.ds(r0, LN_ROWS)
            hbuf[rows, :] = _norm_rows(_f32(xbuf[k, rows, :]), gain, bias)

        @pl.when(k == 0)
        def _():
            wait_weights((0, 1), (0, 1))

        for c0 in range(0, 2 * qkv_w, QKV_CHUNK):
            grp, off = c0 // qkv_w, c0 % qkv_w
            cols = pl.ds(c0, QKV_CHUNK)
            if off + QKV_CHUNK <= qkv_w:
                add = _f32(bqkv[grp, :, pl.ds(off, QKV_CHUNK)])
            else:
                add = jnp.concatenate([_f32(bqkv[grp, :, pl.ds(off, qkv_w - off)]), _f32(bqkv[grp + 1, :, pl.ds(0, QKV_CHUNK - (qkv_w - off))])], axis=1)
            qkv[:, cols] = (_dot(hbuf[...], wqkv[:, cols]) + add).astype(jnp.bfloat16)

        @pl.when(k >= 2)
        def _():
            for grp in range(2):
                o_copy(slot, grp).wait_send()

        lane_head = lax.broadcasted_iota(jnp.int32, (seq, group_w), 1)
        masks = [(lane_head >= hd * head_dim) & (lane_head < (hd + 1) * head_dim) for hd in range(group_heads)]
        causal = row_id >= col_id
        for grp in range(2):
            q = qkv[:, pl.ds(grp * qkv_w, group_w)]
            key = qkv[:, pl.ds(grp * qkv_w + group_w, group_w)]
            val = qkv[:, pl.ds(grp * qkv_w + 2 * group_w, group_w)]
            zero = jnp.zeros_like(q)
            q_heads = jnp.concatenate([jnp.where(m, q, zero) for m in masks], axis=0)
            scores = lax.dot_general(q_heads, key, (((1,), (1,)), ((), ())), preferred_element_type=jnp.float32)
            probs = []
            for hd in range(group_heads):
                sc = jnp.where(causal, scores[hd * seq:(hd + 1) * seq] * (head_dim ** -0.5), -1e30)
                ex = jnp.exp(sc - jnp.max(sc, axis=-1, keepdims=True))
                probs.append((ex / jnp.sum(ex, axis=-1, keepdims=True)).astype(jnp.bfloat16))
            v_heads = jnp.concatenate([jnp.where(m, val, zero) for m in masks], axis=0)
            o_grp = _dot(jnp.concatenate(probs, axis=1), v_heads)
            obuf[slot, side, :, pl.ds(grp * group_w, group_w)] = o_grp.astype(jnp.bfloat16)
            o_copy(slot, grp).start()

    def mlp(k):
        slot = k % 2

        @pl.when(k == 0)
        def _():
            wait_weights((2,), (2, 3, 4))

        for c0 in range(0, d_model, OUT_CHUNK):
            cols = pl.ds(c0, OUT_CHUNK)
            acc[:, cols] = _dot(obuf[slot, side, :, pl.ds(0, group_w * 2)], jnp.concatenate([wout[2 * side, :, cols], wout[2 * side + 1, :, cols]], axis=0))
        for grp in range(2):
            o_copy(slot, grp).wait_recv()
        oth = 1 - side
        for c0 in range(0, d_model, OUT_CHUNK):
            cols = pl.ds(c0, OUT_CHUNK)
            part = _dot(obuf[slot, oth, :, pl.ds(0, group_w * 2)], jnp.concatenate([wout[2 * oth, :, cols], wout[2 * oth + 1, :, cols]], axis=0))
            att = ((acc[:, cols] + part) + _f32(b_out[:, cols])).astype(jnp.bfloat16)
            x1buf[:, cols] = (_f32(xbuf[k, :, cols]) + _f32(att)).astype(jnp.bfloat16)

        gain, bias = _f32(ln2_gain[...]), _f32(ln2_bias[...])
        for r0 in range(0, seq, LN_ROWS):
            rows = pl.ds(r0, LN_ROWS)
            hbuf[rows, :] = _norm_rows(_f32(x1buf[rows, :]), gain, bias)

        @pl.when(k == 0)
        def _():
            wait_weights((3, 4), (5, 6))

        for grp in range(2):
            for c0 in range(0, ff, UP_CHUNK):
                cols = pl.ds(c0, UP_CHUNK)
                pre = _dot(hbuf[...], wup[grp, :, cols]) + _f32(bup[grp, :, cols])
                ubuf[grp, :, cols] = jax.nn.gelu(pre, approximate=True).astype(jnp.bfloat16)

        @pl.when(k == 0)
        def _():
            wait_weights((5,), (7,))

        @pl.when(k >= 2)
        def _():
            for idx in range(p_chunks):
                p_copy(slot, idx).wait_send()

        for idx in range(p_chunks):
            cols = pl.ds(idx * DOWN_CHUNK, DOWN_CHUNK)
            part = _dot(ubuf[0], wdn[0, :, cols]) + _dot(ubuf[1], wdn[1, :, cols])
            pown[slot, :, cols] = part.astype(jnp.bfloat16)
            p_copy(slot, idx).start()

    def finish(k):
        slot = k % 2

        @pl.when(k >= 2)
        def _():
            y_wait(k - 2, slot)

        for idx in range(p_chunks):
            cols = pl.ds(idx * DOWN_CHUNK, DOWN_CHUNK)
            p_copy(slot, idx).wait_recv()
            both = (_f32(pown[slot, :, cols]) + _f32(prcv[slot, :, cols])) + _f32(b_down[:, cols])
            ybuf[slot, :, cols] = (_f32(x1buf[:, cols]) + _f32(both.astype(jnp.bfloat16))).astype(jnp.bfloat16)
        y_start(k, slot)

    def step(k, carry):
        attention(k)

        @pl.when(k >= 1)
        def _():
            finish(k - 1)

        mlp(k)
        return carry

    lax.fori_loop(0, units, step, 0)
    finish(units - 1)

    for k in range(max(units - 2, 0), units):
        slot = k % 2
        for grp in range(2):
            o_copy(slot, grp).wait_send()
        for idx in range(p_chunks):
            p_copy(slot, idx).wait_send()
        y_wait(k, slot)

        @pl.when(diag_recv)
        def _():
            wb_copy(k, slot).wait_send()

    for copy in passes:
        copy.wait_send()

    def wait_y(k, carry):
        y_twin(k, 0).wait_recv()
        return carry

    lax.fori_loop(0, units, wait_y, 0)


def solution(mesh):
    stages = mesh.shape["pp"]
    weight_specs = (
        P('pp', None), P('pp', None),
        P('pp', None, None, 'tp', None), P('pp', None, 'tp', None),
        P('pp', 'tp', None, None), P('pp', None),
        P('pp', None), P('pp', None),
        P('pp', None, 'tp'), P('pp', 'tp'),
        P('pp', 'tp', None), P('pp', None),
    )
    if mesh.shape["tp"] != 4 or stages % 2:
        raise ValueError("unsupported mesh")

    def local_run(x_micro, ln1_gain, ln1_bias, w_qkv, b_qkv, w_out, b_out, ln2_gain, ln2_bias, w_up, b_up, w_down, b_down):
        micro, rows, seq, d_model = x_micro.shape
        total = micro * rows
        units = total // 2
        _, _, _, heads, head_dim = w_qkv.shape
        group_w = heads * head_dim
        ff = w_up.shape[-1]
        x_seqs = x_micro.reshape(total, seq, d_model)
        w_qkv = jnp.transpose(w_qkv[0], (1, 0, 2, 3)).reshape(d_model, 3 * group_w)
        b_qkv = b_qkv.reshape(1, 3 * group_w)
        w_out = w_out.reshape(group_w, d_model)
        any_spec = pl.BlockSpec(memory_space=pl.ANY)
        vmem_spec = pl.BlockSpec(memory_space=pltpu.VMEM)
        bf16, dma = jnp.bfloat16, pltpu.SemaphoreType.DMA
        p_chunks = d_model // DOWN_CHUNK
        y_all = pl.pallas_call(
            functools.partial(_pipeline_kernel, stages, head_dim),
            out_shape=jax.ShapeDtypeStruct((total, seq, d_model), bf16),
            in_specs=[any_spec] * 5 + [any_spec] * 2 + [vmem_spec] * 6,
            out_specs=any_spec,
            scratch_shapes=[
                pltpu.VMEM((d_model, 6 * group_w), bf16),
                pltpu.VMEM((4, group_w, d_model), bf16),
                pltpu.VMEM((2, d_model, ff), bf16),
                pltpu.VMEM((2, ff, d_model), bf16),
                pltpu.VMEM((2, 1, 3 * group_w), bf16),
                pltpu.VMEM((2, 1, ff), bf16),
                pltpu.VMEM((units, seq, d_model), bf16),
                pltpu.VMEM((seq, d_model), bf16),
                pltpu.VMEM((seq, 6 * group_w), bf16),
                pltpu.VMEM((2, 2, seq, 2 * group_w), bf16),
                pltpu.VMEM((seq, d_model), jnp.float32),
                pltpu.VMEM((seq, d_model), bf16),
                pltpu.VMEM((2, seq, ff), bf16),
                pltpu.VMEM((2, seq, d_model), bf16),
                pltpu.VMEM((2, seq, d_model), bf16),
                pltpu.VMEM((2, seq, d_model), bf16),
                dma((units,)), dma((units,)),
                dma((6,)), dma((8,)), dma((8,)),
                dma((2, 2)), dma((2, 2)),
                dma((2, p_chunks)), dma((2, p_chunks)),
                dma((2,)), dma((2,)), dma((2,)), dma((2,)),
            ],
            compiler_params=pltpu.CompilerParams(collective_id=0, has_side_effects=True, vmem_limit_bytes=60 * 1024 * 1024),
            name="stage_pipeline",
        )(x_seqs, w_qkv, w_out, w_up.reshape(d_model, ff), w_down.reshape(ff, d_model), b_qkv, b_up,
          ln1_gain, ln1_bias, b_out, ln2_gain, ln2_bias, b_down)
        return y_all.reshape(1, micro, rows, seq, d_model)

    return jax.shard_map(local_run, mesh=mesh, in_specs=(P(None, 'dp', None, None),) + weight_specs, out_specs=P('pp', None, 'dp', None, None), check_vma=False)
```

time: 2840 us -> 753 us (0.27)
  waiting for transfers between devices: 2090 us -> 0 us
  Pallas kernels: 0 us -> 729 us
  matrix products: 405 us -> 0 us
  other arithmetic: 201 us -> 0 us
  local copies, waits for them, and re-layouts: 82.7 us -> 23.9 us
    psum x30 -> x0, waiting for transfers between devices: 2000 us -> none  [the longest x15 1190 us: stage_layer(): lax.psum(attn_part, 'tp').astype(jnp.float32) + b_out.astype(jnp.float32)]
    pallas_call x0 -> x1, Pallas kernels: none -> 729 us  [local_run(): pl.pallas_call(functools.partial(_pipeline_kernel, stages, head_dim), out...]
    dot_general x60 -> x0, matrix products: 359 us -> none  [the longest x15 127 us: stage_layer(): jnp.einsum('bsd,df->bsf', normed_mid, w_up, preferred_element_type=jnp.fl...]
    reduce_sum x60 -> x0, other arithmetic: 111 us -> none  [the longest x30 87.9 us: layer_norm(): row_mean = jnp.mean(act_f32, axis=-1, keepdims=True)]
    dynamic_update_slice x15 -> x0, other arithmetic: 84.5 us -> none  [time_step(): lax.dynamic_update_index_in_dim(out_buf, jnp.where(is_valid, stage_out, o...]
    ppermute x15 -> x0, waiting for transfers between devices: 83.5 us -> none  [time_step(): received = lax.ppermute(stage_out, 'pp', shift_pairs)]
    dynamic_slice x15 -> x0, local copies, waits for them, and re-layouts: 52.7 us -> none  [time_step(): old_slot = lax.dynamic_index_in_dim(out_buf, slot_idx, 0, keepdims=False)]
    sub x15 -> x0, matrix products: 46.4 us -> none  [stage_layer(): jax.nn.softmax(jnp.where(causal, scores, -1e+30), axis=-1)]
  transfers between devices with their start and end apart: 45 -> 0, of which waited for: 45 -> 0; matrix products, arithmetic and copies ran while one was open for 2% -> 0% of each run, Pallas kernels for 0% -> 0%
where the time goes in v1:
time: 753 us
  Pallas kernels  729 us (97%)
  local copies, waits for them, and re-layouts  23.9 us (3%)
    pallas_call x1, Pallas kernels, local_run(): pl.pallas_call(functools.partial(_pipeline_kernel, stages, head_dim), out...  729 us
    unnamed x1, local copies, waits for them, and re-layouts  16.9 us

profile of v1, /device:TPU:103, one launch (start us, length us, event | category | flops | bytes accessed | tf_op | source)
XLA Modules:
  0.0 752.5 jit_solution(4898951096753076215)
XLA Ops:
  0.0 1.4 reshape.26.bqkv_in
  1.4 5.7 copy.15.wqkv_hbm
  7.1 728.6 %stage_pipeline.1 = bf16[48,128,1536]{2,1,0:T(8,128)(2,1)} custom-call(bf16[48,128,1536]{2,1,0:T(8,128)(2,1)} %bitcast.11, bf16[1536,1152]{1,0:T(8,128)(2,1)} %copy.15.wqkv_hbm, bf16[384,1536]{1,0:T(8,128)(2,1)} %bitcast.15, bf16[1536,1536]{1,0:T(8,128)(2,1)} %bitcast.12, bf16[1536,1536]{1,0:T(8,128)(2,1)} %bitcast.13, bf16[1,1152]{1,0:T(2,128)(2,1)} %reshape.26.bqkv_in, ...), custom_call_target="tpu_custom_call" | custom-call | tf_op jit(solution)/shard_map/stage_pipeline/pallas_call | solution.py:380
  735.7 16.9 %copy.17 = bf16[1,8,6,128,1536]{4,3,2,1,0:T(8,128)(2,1)} copy(bf16[1,8,6,128,1536]{4,3,2,1,0:T(8,128)(2,1)} %bitcast.10) | data formatting | bytes 37748736

commit v2 on v1

--- a/solution.py
+++ b/solution.py
@@ -14,6 +14,7 @@
 DOWN_CHUNK = 512
 OUT_CHUNK = 512
 QKV_CHUNK = 768
+RELAY_STEPS = 16
 
 
 def _f32(val):
@@ -36,7 +37,8 @@
                      ln1_gain, ln1_bias, b_out, ln2_gain, ln2_bias, b_down,
                      y_hbm,
                      wqkv, wout, wup, wdn, bqkv, bup, xbuf, hbuf, qkv, obuf, acc, x1buf, ubuf, pown, prcv, ybuf,
-                     x_sem, yr_sem, wl_sem, ws_sem, wr_sem, os_sem, or_sem, ps_sem, pr_sem, yl_sem, yn_sem, ye_sem, wb_sem):
+                     x_sem, yr_sem, wl_sem, ws_sem, wr_sem, os_sem, or_sem, ps_sem, pr_sem, yl_sem, yn_sem, ye_sem, wb_sem,
+                     relay_a, relay_b, ra_sem, rb_sem, hop_sem):
     units, seq, d_model = xbuf.shape
     group_w = wout_hbm.shape[0]
     group_heads = group_w // head_dim
@@ -55,6 +57,8 @@
     half = odd_type * (rr // 2) + even_type * (((rr + 1) // 2) % 2)
     base = half * units
     has_next = pp + 1 < stages
+    lender = pp < stages // 2
+    ally = stages - 2 - pp + 2 * (pp % 2)
     diag_send = (pp % 2 == 0) & (rr % 2 == 0)
     diag_recv = (pp % 2 == 1) & (rr % 2 == 1)
 
@@ -78,7 +82,7 @@
         remote(bqkv_in, bqkv.at[1], ws_sem.at[1], wr_sem.at[1], {"tp": twin}),
         remote(wout_hbm, wout.at[2 * twin_side + 1], ws_sem.at[2], wr_sem.at[2], {"tp": twin}),
         remote(wout_hbm, wout.at[2 * side], ws_sem.at[3], wr_sem.at[3], {"tp": mate}),
-        remote(wout_hbm, wout.at[2 * twin_side + 1], ws_sem.at[4], wr_sem.at[4], {"tp": cross}),
+        remote(wout.at[2 * side + 1], wout.at[2 * side + 1], ws_sem.at[4], wr_sem.at[4], {"tp": mate}),
         remote(wup_hbm, wup.at[1], ws_sem.at[5], wr_sem.at[5], {"tp": twin}),
         remote(bup_in, bup.at[1], ws_sem.at[6], wr_sem.at[6], {"tp": twin}),
         remote(wdn_hbm, wdn.at[1], ws_sem.at[7], wr_sem.at[7], {"tp": twin}),
@@ -126,10 +130,58 @@
 
     diag_count = (1 - (pp % 2)) * (1 - (rr % 2)) + (pp % 2) * (rr % 2)
     inner = jnp.where(has_next, 1, 0) + jnp.where(pp > 0, 1, 0)
-    pl.semaphore_wait(barrier, 3 + inner + diag_count)
-
-    for copy in passes:
-        copy.start()
+    greet({"pp": ally})
+    pl.semaphore_wait(barrier, 4 + inner + diag_count)
+
+    for idx in (2, 0, 1, 5, 6):
+        passes[idx].start()
+
+    steps = RELAY_STEPS
+    part = ff // steps
+
+    def relay_rows(c):
+        return pl.ds(c * part, part)
+
+    def hop_in(c):
+        return remote(wdn_hbm.at[relay_rows(c)], relay_a.at[relay_rows(c)], ws_sem.at[7], ra_sem.at[c], {"pp": ally})
+
+    def hop_over(c):
+        return remote(relay_a.at[relay_rows(c)], relay_b.at[relay_rows(c)], hop_sem.at[0], rb_sem.at[c], {"tp": mate})
+
+    def hop_out(c):
+        return remote(relay_b.at[relay_rows(c)], wdn.at[1, relay_rows(c)], hop_sem.at[1], wr_sem.at[7], {"pp": ally})
+
+    @pl.when(lender)
+    def _():
+        def lend(c, carry):
+            hop_in(c).start()
+            return carry
+        lax.fori_loop(0, steps, lend, 0)
+        passes[3].start()
+        passes[2].wait_recv()
+        passes[4].start()
+
+    @pl.when(jnp.logical_not(lender))
+    def _():
+        passes[7].start()
+
+    @pl.when(jnp.logical_not(lender))
+    def _():
+        def relay(c, carry):
+            @pl.when(c < steps)
+            def _():
+                hop_in(c).wait_recv()
+                hop_over(c).start()
+
+            @pl.when(c >= 1)
+            def _():
+                hop_over(c - 1).wait_recv()
+                hop_out(c - 1).start()
+            return carry
+        lax.fori_loop(0, steps + 1, relay, 0)
+        passes[3].start()
+        passes[2].wait_recv()
+        passes[4].start()
 
     def wait_weights(load_idx, pass_idx):
         for idx in load_idx:
@@ -153,46 +205,45 @@
     def y_local(k, slot):
         return local(ybuf.at[slot], y_hbm.at[base + k], yl_sem.at[slot])
 
-    def y_next(k, slot):
-        return remote(ybuf.at[slot], xbuf.at[k], yn_sem.at[slot], x_sem.at[k], {"pp": pp + 1})
-
-    def y_twin(k, slot):
-        return remote(ybuf.at[slot], y_hbm.at[base + k], ye_sem.at[slot], yr_sem.at[k], {"tp": twin})
-
-    def y_diag(k, slot):
-        return remote(ybuf.at[slot], xbuf.at[k], ye_sem.at[slot], x_sem.at[k], {"tp": twin, "pp": pp + 1})
+    def y_next(k, slot, cols):
+        return remote(ybuf.at[slot, :, cols], xbuf.at[k, :, cols], yn_sem.at[slot], x_sem.at[k], {"pp": pp + 1})
+
+    def y_twin(k, slot, cols):
+        return remote(ybuf.at[slot, :, cols], y_hbm.at[base + k, :, cols], ye_sem.at[slot], yr_sem.at[k], {"tp": twin})
+
+    def y_diag(k, slot, cols):
+        return remote(ybuf.at[slot, :, cols], xbuf.at[k, :, cols], ye_sem.at[slot], x_sem.at[k], {"tp": twin, "pp": pp + 1})
 
     sends_next = has_next & ((pp % 2 == 1) | (rr % 2 == 0))
-
-    def y_start(k, slot):
-        y_local(k, slot).start()
-
+    all_cols = pl.ds(0, d_model)
+
+    def y_start(k, slot, cols):
         @pl.when(sends_next)
         def _():
-            y_next(k, slot).start()
+            y_next(k, slot, cols).start()
 
         @pl.when(diag_send)
         def _():
-            y_diag(k, slot).start()
+            y_diag(k, slot, cols).start()
 
         @pl.when(jnp.logical_not(diag_send))
         def _():
-            y_twin(k, slot).start()
+            y_twin(k, slot, cols).start()
 
     def y_wait(k, slot):
         y_local(k, slot).wait()
 
         @pl.when(sends_next)
         def _():
-            y_next(k, slot).wait_send()
+            y_next(k, slot, all_cols).wait_send()
 
         @pl.when(diag_send)
         def _():
-            y_diag(k, slot).wait_send()
+            y_diag(k, slot, all_cols).wait_send()
 
         @pl.when(jnp.logical_not(diag_send))
         def _():
-            y_twin(k, slot).wait_send()
+            y_twin(k, slot, all_cols).wait_send()
 
     def wb_copy(k, slot):
         return remote(xbuf.at[k], y_hbm.at[base + k], wb_sem.at[slot], yr_sem.at[k], {"pp": pp - 1})
@@ -256,7 +307,7 @@
 
         @pl.when(k == 0)
         def _():
-            wait_weights((2,), (2, 3, 4))
+            wait_weights((2,), (3, 4))
 
         for c0 in range(0, d_model, OUT_CHUNK):
             cols = pl.ds(c0, OUT_CHUNK)
@@ -268,12 +319,12 @@
             cols = pl.ds(c0, OUT_CHUNK)
             part = _dot(obuf[slot, oth, :, pl.ds(0, group_w * 2)], jnp.concatenate([wout[2 * oth, :, cols], wout[2 * oth + 1, :, cols]], axis=0))
             att = ((acc[:, cols] + part) + _f32(b_out[:, cols])).astype(jnp.bfloat16)
-            x1buf[:, cols] = (_f32(xbuf[k, :, cols]) + _f32(att)).astype(jnp.bfloat16)
+            x1buf[slot, :, cols] = (_f32(xbuf[k, :, cols]) + _f32(att)).astype(jnp.bfloat16)
 
         gain, bias = _f32(ln2_gain[...]), _f32(ln2_bias[...])
         for r0 in range(0, seq, LN_ROWS):
             rows = pl.ds(r0, LN_ROWS)
-            hbuf[rows, :] = _norm_rows(_f32(x1buf[rows, :]), gain, bias)
+            hbuf[rows, :] = _norm_rows(_f32(x1buf[slot, rows, :]), gain, bias)
 
         @pl.when(k == 0)
         def _():
@@ -311,20 +362,29 @@
             cols = pl.ds(idx * DOWN_CHUNK, DOWN_CHUNK)
             p_copy(slot, idx).wait_recv()
             both = (_f32(pown[slot, :, cols]) + _f32(prcv[slot, :, cols])) + _f32(b_down[:, cols])
-            ybuf[slot, :, cols] = (_f32(x1buf[:, cols]) + _f32(both.astype(jnp.bfloat16))).astype(jnp.bfloat16)
-        y_start(k, slot)
-
-    def step(k, carry):
-        attention(k)
-
-        @pl.when(k >= 1)
-        def _():
-            finish(k - 1)
-
-        mlp(k)
+            ybuf[slot, :, cols] = (_f32(x1buf[slot, :, cols]) + _f32(both.astype(jnp.bfloat16))).astype(jnp.bfloat16)
+            y_start(k, slot, cols)
+        y_local(k, slot).start()
+
+    def step(i, carry):
+        def attention_pair(par, inner):
+            attention(2 * i + par)
+
+            @pl.when((par == 0) & (i >= 1))
+            def _():
+                finish(2 * i - 1)
+            return inner
+
+        def mlp_pair(par, inner):
+            mlp(2 * i + par)
+            return inner
+
+        lax.fori_loop(0, 2, attention_pair, 0)
+        lax.fori_loop(0, 2, mlp_pair, 0)
+        finish(2 * i)
         return carry
 
-    lax.fori_loop(0, units, step, 0)
+    lax.fori_loop(0, units // 2, step, 0)
     finish(units - 1)
 
     for k in range(max(units - 2, 0), units):
@@ -342,8 +402,13 @@
     for copy in passes:
         copy.wait_send()
 
+    @pl.when(jnp.logical_not(lender))
+    def _():
+        remote(relay_a, relay_b, hop_sem.at[0], rb_sem.at[0], {"tp": mate}).wait_send()
+        remote(relay_b, wdn.at[1], hop_sem.at[1], wr_sem.at[7], {"pp": ally}).wait_send()
+
     def wait_y(k, carry):
-        y_twin(k, 0).wait_recv()
+        y_twin(k, 0, all_cols).wait_recv()
         return carry
 
     lax.fori_loop(0, units, wait_y, 0)
@@ -359,7 +424,7 @@
         P('pp', None, 'tp'), P('pp', 'tp'),
         P('pp', 'tp', None), P('pp', None),
     )
-    if mesh.shape["tp"] != 4 or stages % 2:
+    if mesh.shape["tp"] != 4 or stages % 4:
         raise ValueError("unsupported mesh")
 
     def local_run(x_micro, ln1_gain, ln1_bias, w_qkv, b_qkv, w_out, b_out, ln2_gain, ln2_bias, w_up, b_up, w_down, b_down):
@@ -394,7 +459,7 @@
                 pltpu.VMEM((seq, 6 * group_w), bf16),
                 pltpu.VMEM((2, 2, seq, 2 * group_w), bf16),
                 pltpu.VMEM((seq, d_model), jnp.float32),
-                pltpu.VMEM((seq, d_model), bf16),
+                pltpu.VMEM((2, seq, d_model), bf16),
                 pltpu.VMEM((2, seq, ff), bf16),
                 pltpu.VMEM((2, seq, d_model), bf16),
                 pltpu.VMEM((2, seq, d_model), bf16),
@@ -404,6 +469,9 @@
                 dma((2, 2)), dma((2, 2)),
                 dma((2, p_chunks)), dma((2, p_chunks)),
                 dma((2,)), dma((2,)), dma((2,)), dma((2,)),
+                pltpu.VMEM((ff, d_model), bf16),
+                pltpu.VMEM((ff, d_model), bf16),
+                dma((RELAY_STEPS,)), dma((RELAY_STEPS,)), dma((2,)),
             ],
             compiler_params=pltpu.CompilerParams(collective_id=0, has_side_effects=True, vmem_limit_bytes=60 * 1024 * 1024),
             name="stage_pipeline",

time: 753 us -> 634 us (0.84)
  Pallas kernels: 729 us -> 610 us
    pallas_call x1, Pallas kernels: 729 us -> 610 us  [local_run(): pl.pallas_call(functools.partial(_pipeline_kernel, stages, head_dim), out...]
where the time goes in v2:
time: 634 us
  Pallas kernels  610 us (96%)
  local copies, waits for them, and re-layouts  23.9 us (4%)
    pallas_call x1, Pallas kernels, local_run(): pl.pallas_call(functools.partial(_pipeline_kernel, stages, head_dim), out...  610 us
    unnamed x1, local copies, waits for them, and re-layouts  16.9 us

profile of v2, /device:TPU:103, one launch (start us, length us, event | category | flops | bytes accessed | tf_op | source)
XLA Modules:
  0.0 633.8 jit_solution(18375751676846187665)
XLA Ops:
  0.0 1.4 reshape.26.bqkv_in
  1.4 5.7 copy.15.wqkv_hbm
  7.1 609.8 %stage_pipeline.1 = bf16[48,128,1536]{2,1,0:T(8,128)(2,1)} custom-call(bf16[48,128,1536]{2,1,0:T(8,128)(2,1)} %bitcast.11, bf16[1536,1152]{1,0:T(8,128)(2,1)} %copy.15.wqkv_hbm, bf16[384,1536]{1,0:T(8,128)(2,1)} %bitcast.15, bf16[1536,1536]{1,0:T(8,128)(2,1)} %bitcast.12, bf16[1536,1536]{1,0:T(8,128)(2,1)} %bitcast.13, bf16[1,1152]{1,0:T(2,128)(2,1)} %reshape.26.bqkv_in, ...), custom_call_target="tpu_custom_call" | custom-call | tf_op jit(solution)/shard_map/stage_pipeline/pallas_call | solution.py:445
  616.9 16.9 %copy.17 = bf16[1,8,6,128,1536]{4,3,2,1,0:T(8,128)(2,1)} copy(bf16[1,8,6,128,1536]{4,3,2,1,0:T(8,128)(2,1)} %bitcast.10) | data formatting | bytes 37748736

commit v3 on v2

v3 whole, which is shorter than its diff:
```python
import functools

import jax
import jax.numpy as jnp
from jax import lax
from jax.experimental import pallas as pl
from jax.experimental.pallas import tpu as pltpu
from jax.sharding import PartitionSpec as P

LN_EPS = 1e-5
MESH = pl.DeviceIdType.MESH
LN_ROWS = 16
UP_CHUNK = 512
DOWN_CHUNK = 512
OUT_CHUNK = 512
RELAY_STEPS = 16
LAGGED_STAGES = 2
EAGER_UNITS = (0, 0, 1, 12)
TURN_ROWS = 128


def _f32(val):
    return val.astype(jnp.float32)


def _norm_rows(rows, gain, bias):
    width = rows.shape[-1]
    mean = jnp.sum(rows, axis=-1, keepdims=True) * (1.0 / width)
    cen = rows - mean
    var = jnp.sum(cen * cen, axis=-1, keepdims=True) * (1.0 / width)
    return (cen * lax.rsqrt(var + LN_EPS) * gain + bias).astype(jnp.bfloat16)


def _dot(lhs, rhs):
    return jnp.dot(lhs, rhs, preferred_element_type=jnp.float32)


def _pipeline_kernel(stages, head_dim, x_hbm, wqkv_hbm, wout_hbm, wup_hbm, wdn_hbm, bqkv_in, bup_in,
                     ln1_gain, ln1_bias, b_out, ln2_gain, ln2_bias, b_down,
                     y_hbm,
                     wqkv, wout, wup, wdn, bqkv, bup, xbuf, hbuf, qkv, obuf, acc, x1buf, ubuf, pown, prcv, ybuf,
                     relay_a, relay_b, turn,
                     x_sem, wl_sem, ws_sem, wr_sem, os_sem, or_sem, ps_sem, pr_sem, yl_sem, yn_sem, yd_sem, ym_sem, ymr_sem, yf_sem, yt_sem, yl_late,
                     wb_sem, ra_sem, rb_sem, hop_sem):
    _, units, seq, d_model = xbuf.shape
    group_w = wout_hbm.shape[0]
    group_heads = group_w // head_dim
    qk_w = 2 * group_w
    v_col = 2 * qk_w
    ff = wup_hbm.shape[1]
    rr = lax.axis_index("tp")
    pp = lax.axis_index("pp")
    odd = pp % 2
    near, far = rr + 1 - 2 * (rr % 2), 3 - rr
    mate = odd * near + (1 - odd) * far
    twin = odd * far + (1 - odd) * near
    has_next = pp + 1 < stages
    has_prev = pp > 0
    lagged = pp >= stages - LAGGED_STAGES
    is_last = pp == stages - 1
    eager = 0
    for quarter, amount in enumerate(EAGER_UNITS):
        eager = eager + jnp.where(pp * len(EAGER_UNITS) // stages == quarter, min(amount, units), 0)
    lender = pp < stages // 2
    ally = stages - 1 - pp
    OWN, MATE = 0, 1

    def local(src, dst, sem):
        return pltpu.make_async_copy(src, dst, sem)

    def remote(src, dst, send, recv, dev):
        return pltpu.make_async_remote_copy(src_ref=src, dst_ref=dst, send_sem=send, recv_sem=recv, device_id=dev, device_id_type=MESH)

    own_qk, twin_qk = pl.ds(0, qk_w), pl.ds(qk_w, qk_w)
    own_v, twin_v = pl.ds(v_col, group_w), pl.ds(v_col + group_w, group_w)
    turn_rows = turn.shape[1]
    turns = 3 * group_w // turn_rows

    def turn_load(c, slot):
        return local(wqkv_hbm.at[pl.ds(c * turn_rows, turn_rows)], turn.at[slot], wl_sem.at[slot])

    loads = [
        local(wout_hbm, wout.at[0], wl_sem.at[2]),
        local(wup_hbm, wup.at[0], wl_sem.at[3]),
        local(bup_in, bup.at[0], wl_sem.at[4]),
        local(wdn_hbm, wdn.at[0], wl_sem.at[5]),
    ]
    to_twin, to_mate = {"tp": twin}, {"tp": mate}
    passes = [
        remote(wqkv.at[:, own_qk], wqkv.at[:, twin_qk], ws_sem.at[0], wr_sem.at[0], to_twin),
        remote(bqkv.at[:, own_qk], bqkv.at[:, twin_qk], ws_sem.at[1], wr_sem.at[1], to_twin),
        remote(wout_hbm, wout.at[1], ws_sem.at[2], wr_sem.at[2], to_twin),
        remote(wout_hbm, wout.at[2], ws_sem.at[3], wr_sem.at[3], to_mate),
        remote(wout.at[1], wout.at[3], ws_sem.at[4], wr_sem.at[4], to_mate),
        remote(wup_hbm, wup.at[1], ws_sem.at[5], wr_sem.at[5], to_twin),
        remote(bup_in, bup.at[1], ws_sem.at[6], wr_sem.at[6], to_twin),
        remote(wdn_hbm, wdn.at[1], ws_sem.at[7], wr_sem.at[7], to_twin),
        remote(wqkv.at[:, own_v], wqkv.at[:, twin_v], ws_sem.at[8], wr_sem.at[8], to_twin),
        remote(bqkv.at[:, own_v], bqkv.at[:, twin_v], ws_sem.at[9], wr_sem.at[9], to_twin),
    ]

    def x_load(kind, i, row):
        return local(x_hbm.at[row * units + i], xbuf.at[kind, i], x_sem.at[kind, i])

    turn_load(0, 0).start()
    turn_load(1, 1).start()

    @pl.when(pp == 0)
    def _():
        def start_x(i, carry):
            x_load(OWN, i, rr).start()
            x_load(MATE, i, mate).start()
            return carry
        lax.fori_loop(0, units, start_x, 0)

    for copy in loads:
        copy.start()

    barrier = pltpu.get_barrier_semaphore()

    def greet(dev):
        pl.semaphore_signal(barrier, inc=1, device_id=dev, device_id_type=MESH)

    greet(to_mate)
    greet(to_twin)
    greet({"pp": ally})

    @pl.when(has_next)
    def _():
        greet({"pp": pp + 1})
        greet({"tp": twin, "pp": pp + 1})

    @pl.when(has_prev)
    def _():
        greet({"pp": pp - 1})
        greet({"tp": mate, "pp": pp - 1})

    pl.semaphore_wait(barrier, 3 + 2 * (jnp.where(has_next, 1, 0) + jnp.where(has_prev, 1, 0)))

    passes[2].start()

    steps = RELAY_STEPS
    part = ff // steps
    lend_some = max(steps // 4, 1)
    lends_all = (pp < stages // 4) | (pp >= stages - stages // 4)
    lent = jnp.where(lends_all, steps, lend_some)

    def relay_rows(c):
        return pl.ds(c * part, part)

    def hop_in(c):
        return remote(wdn_hbm.at[relay_rows(c)], relay_a.at[relay_rows(c)], ws_sem.at[7], ra_sem.at[c], {"pp": ally})

    def hop_over(c):
        return remote(relay_a.at[relay_rows(c)], relay_b.at[relay_rows(c)], hop_sem.at[0], rb_sem.at[c], to_mate)

    def hop_out(c):
        return remote(relay_b.at[relay_rows(c)], wdn.at[1, relay_rows(c)], hop_sem.at[1], wr_sem.at[7], {"pp": ally})

    def direct(c):
        return remote(wdn_hbm.at[relay_rows(c)], wdn.at[1, relay_rows(c)], ws_sem.at[7], wr_sem.at[7], to_twin)

    @pl.when(lender)
    def _():
        def lend(c, carry):
            hop_in(c).start()
            return carry
        lax.fori_loop(0, lent, lend, 0)
        passes[3].start()
        passes[2].wait_recv()
        passes[4].start()

    def turn_block(c, carry):
        slot = c % 2
        turn_load(c, slot).wait()
        first = c * turn_rows
        col = first + (first // qk_w) * (v_col - qk_w)
        wqkv[:, pl.ds(pl.multiple_of(col, 128), turn_rows)] = turn[slot].T

        @pl.when(c + 2 < turns)
        def _():
            turn_load(c + 2, slot).start()
        return carry

    lax.fori_loop(0, turns, turn_block, 0)
    spread_row = lax.broadcasted_iota(jnp.int32, (head_dim, group_w), 0)
    spread_col = lax.broadcasted_iota(jnp.int32, (head_dim, group_w), 1)
    spread = jnp.zeros((head_dim, group_w), jnp.float32)
    for hd in range(group_heads):
        spread = spread + jnp.where(spread_row + hd * head_dim == spread_col, 1.0, 0.0)
    spread = spread.astype(jnp.bfloat16)
    head_row = lax.broadcasted_iota(jnp.int32, (group_heads, group_w), 0)
    head_lane = lax.broadcasted_iota(jnp.int32, (group_heads, group_w), 1)
    in_head = (head_lane >= head_row * head_dim) & (head_lane < (head_row + 1) * head_dim)
    for third in range(3):
        wide = jnp.where(in_head, _dot(bqkv_in[0, third], spread), 0.0)
        col = third * group_w if third < 2 else v_col
        bqkv[:, pl.ds(col, group_w)] = jnp.sum(wide, axis=0, keepdims=True)
    for idx in (0, 8, 1, 9, 5, 6):
        passes[idx].start()

    @pl.when(lender)
    def _():
        def keep(c, carry):
            direct(c).start()
            return carry
        lax.fori_loop(lent, steps, keep, 0)

    @pl.when(jnp.logical_not(lender))
    def _():
        passes[7].start()

        def relay(c, carry):
            @pl.when(c < lent)
            def _():
                hop_in(c).wait_recv()
                hop_over(c).start()

            @pl.when(c >= 1)
            def _():
                hop_over(c - 1).wait_recv()
                hop_out(c - 1).start()
            return carry
        lax.fori_loop(0, lent + 1, relay, 0)
        passes[3].start()
        passes[2].wait_recv()
        passes[4].start()

    def wait_weights(load_idx, pass_idx):
        for idx in load_idx:
            loads[idx].wait()
        for idx in pass_idx:
            passes[idx].wait_recv()

    row_id = lax.broadcasted_iota(jnp.int32, (seq, seq), 0)
    col_id = lax.broadcasted_iota(jnp.int32, (seq, seq), 1)

    def o_copy(kind, slot, grp):
        cols = pl.ds(grp * group_w, group_w)
        return remote(obuf.at[slot, kind, 0, :, cols], obuf.at[slot, 1 - kind, 1, :, cols],
                      os_sem.at[slot, kind, grp], or_sem.at[slot, 1 - kind, grp], to_mate)

    def p_copy(slot, idx):
        cols = pl.ds(idx * DOWN_CHUNK, DOWN_CHUNK)
        return remote(pown.at[MATE, :, cols], prcv.at[slot, :, cols], ps_sem.at[idx], pr_sem.at[slot, idx], to_mate)

    p_chunks = d_model // DOWN_CHUNK
    all_cols = pl.ds(0, d_model)

    def y_local(i, slot):
        return local(ybuf.at[slot], y_hbm.at[rr * units + i], yl_sem.at[slot])

    def y_next(i, slot, cols):
        return remote(ybuf.at[slot, :, cols], xbuf.at[OWN, i, :, cols], yn_sem.at[slot], x_sem.at[OWN, i], {"pp": pp + 1})

    def y_diag(i, slot, cols):
        return remote(ybuf.at[slot, :, cols], xbuf.at[MATE, i, :, cols], yd_sem.at[slot], x_sem.at[MATE, i], {"tp": twin, "pp": pp + 1})

    def y_twin(i, slot, cols):
        return remote(ybuf.at[slot, :, cols], y_hbm.at[rr * units + i, :, cols], yd_sem.at[slot], yt_sem.at[i], to_twin)

    def y_mate(i, slot):
        return remote(ybuf.at[slot], y_hbm.at[rr * units + i], ym_sem.at[slot], ymr_sem.at[i], to_mate)

    def y_mate_late(i):
        ref = y_hbm.at[rr * units + i]
        return remote(ref, ref, yl_late.at[i], ymr_sem.at[i], to_mate)

    def y_forward_mate(i):
        ref = y_hbm.at[mate * units + i]
        return remote(ref, ref, yf_sem.at[0], yf_sem.at[1], to_twin)

    def y_forward_twin(i):
        ref = y_hbm.at[twin * units + i]
        return remote(ref, ref, yf_sem.at[0], yf_sem.at[1], to_mate)

    def twin_arrival(i):
        ref = y_hbm.at[twin * units + i]
        return remote(ref, ref, yd_sem.at[0], yt_sem.at[i], to_twin)

    def y_forward(i):
        by_mate = is_last & (i % 2 == 0)

        @pl.when(by_mate)
        def _():
            twin_arrival(i).wait_recv()
            y_forward_twin(i).start()

        @pl.when(jnp.logical_not(by_mate))
        def _():
            y_mate_late(i).wait_recv()
            y_forward_mate(i).start()

    def y_start(i, slot, cols):
        @pl.when(has_next)
        def _():
            y_next(i, slot, cols).start()
            y_diag(i, slot, cols).start()

        @pl.when(jnp.logical_not(has_next))
        def _():
            y_twin(i, slot, cols).start()

    def y_wait(i, slot):
        y_local(i, slot).wait()

        @pl.when(has_next)
        def _():
            y_next(i, slot, all_cols).wait_send()
            y_diag(i, slot, all_cols).wait_send()

        @pl.when(jnp.logical_not(has_next))
        def _():
            y_twin(i, slot, all_cols).wait_send()

        @pl.when(i < eager)
        def _():
            y_mate(i, slot).wait_send()

    def wb_copy(i, slot):
        return remote(xbuf.at[MATE, i], y_hbm.at[mate * units + i], wb_sem.at[slot], yt_sem.at[i], {"pp": pp - 1})

    def attention(kind, i):
        slot = i % 2
        x_load(kind, i, rr).wait()

        @pl.when((kind == MATE) & has_prev)
        def _():
            @pl.when(i >= 2)
            def _():
                wb_copy(i - 2, slot).wait_send()
            wb_copy(i, slot).start()

        @pl.when((kind == OWN) & (i == 0))
        def _():
            wait_weights((), (0, 1, 8, 9))

        @pl.when(i >= 2)
        def _():
            for grp in range(2):
                o_copy(kind, slot, grp).wait_send()

        gain, bias = _f32(ln1_gain[...]), _f32(ln1_bias[...])
        for r0 in range(0, seq, LN_ROWS):
            rows = pl.ds(r0, LN_ROWS)
            hbuf[rows, :] = _norm_rows(_f32(xbuf[kind, i, rows, :]), gain, bias)

        lane_head = lax.broadcasted_iota(jnp.int32, (seq, group_w), 1)
        masks = [(lane_head >= hd * head_dim) & (lane_head < (hd + 1) * head_dim) for hd in range(group_heads)]
        causal = row_id >= col_id

        def project(col):
            cols = pl.ds(col, qk_w)
            qkv[:, cols] = (_dot(hbuf[...], wqkv[:, cols]) + bqkv[:, cols]).astype(jnp.bfloat16)

        def by_head(act):
            zero = jnp.zeros_like(act)
            return jnp.concatenate([jnp.where(m, act, zero) for m in masks], axis=0)

        def scores_of(grp):
            q_heads = by_head(qkv[:, pl.ds(grp * qk_w, group_w)])
            key = qkv[:, pl.ds(grp * qk_w + group_w, group_w)]
            return lax.dot_general(q_heads, key, (((1,), (1,)), ((), ())), preferred_element_type=jnp.float32)

        def probs_of(scores):
            probs = []
            for hd in range(group_heads):
                sc = jnp.where(causal, scores[hd * seq:(hd + 1) * seq] * (head_dim ** -0.5), -1e30)
                ex = jnp.exp(sc - jnp.max(sc, axis=-1, keepdims=True))
                probs.append((ex * (1.0 / jnp.sum(ex, axis=-1, keepdims=True))).astype(jnp.bfloat16))
            return jnp.concatenate(probs, axis=1)

        project(0)
        scores_0 = scores_of(0)
        project(qk_w)
        probs_0 = probs_of(scores_0)
        scores_1 = scores_of(1)
        project(v_col)
        probs_1 = probs_of(scores_1)
        for grp, probs in enumerate((probs_0, probs_1)):
            val = qkv[:, pl.ds(v_col + grp * group_w, group_w)]
            obuf[slot, kind, 0, :, pl.ds(grp * group_w, group_w)] = _dot(probs, by_head(val)).astype(jnp.bfloat16)
            o_copy(kind, slot, grp).start()

    def mlp(kind, i):
        slot = i % 2
        if kind == MATE:
            @pl.when(i == 0)
            def _():
                wait_weights((0,), (3, 4))

        def out_part(half, cols):
            return _dot(obuf[slot, kind, half], jnp.concatenate([wout[2 * half, :, cols], wout[2 * half + 1, :, cols]], axis=0))

        for c0 in range(0, d_model, OUT_CHUNK):
            cols = pl.ds(c0, OUT_CHUNK)
            acc[:, cols] = out_part(0, cols)
        for grp in range(2):
            o_copy(1 - kind, slot, grp).wait_recv()
        for c0 in range(0, d_model, OUT_CHUNK):
            cols = pl.ds(c0, OUT_CHUNK)
            att = ((acc[:, cols] + out_part(1, cols)) + _f32(b_out[:, cols])).astype(jnp.bfloat16)
            x1buf[:, cols] = (_f32(xbuf[kind, i, :, cols]) + _f32(att)).astype(jnp.bfloat16)

        gain, bias = _f32(ln2_gain[...]), _f32(ln2_bias[...])
        for r0 in range(0, seq, LN_ROWS):
            rows = pl.ds(r0, LN_ROWS)
            hbuf[rows, :] = _norm_rows(_f32(x1buf[rows, :]), gain, bias)

        if kind == MATE:
            @pl.when(i == 0)
            def _():
                wait_weights((1, 2), (5, 6))

        for grp in range(2):
            for c0 in range(0, ff, UP_CHUNK):
                cols = pl.ds(c0, UP_CHUNK)
                pre = _dot(hbuf[...], wup[grp, :, cols]) + _f32(bup[grp, :, cols])
                ubuf[grp, :, cols] = jax.nn.gelu(pre, approximate=True).astype(jnp.bfloat16)

        if kind == MATE:
            @pl.when(i == 0)
            def _():
                wait_weights((3,), (7,))

            @pl.when(i >= 1)
            def _():
                for idx in range(p_chunks):
                    p_copy(slot, idx).wait_send()

        for idx in range(p_chunks):
            cols = pl.ds(idx * DOWN_CHUNK, DOWN_CHUNK)
            pown[kind, :, cols] = (_dot(ubuf[0], wdn[0, :, cols]) + _dot(ubuf[1], wdn[1, :, cols])).astype(jnp.bfloat16)
            if kind == MATE:
                p_copy(slot, idx).start()

    def finish(i):
        slot = i % 2

        @pl.when(i >= 2)
        def _():
            y_wait(i - 2, slot)

        for idx in range(p_chunks):
            cols = pl.ds(idx * DOWN_CHUNK, DOWN_CHUNK)
            p_copy(slot, idx).wait_recv()
            both = (_f32(pown[OWN, :, cols]) + _f32(prcv[slot, :, cols])) + _f32(b_down[:, cols])
            ybuf[slot, :, cols] = (_f32(x1buf[:, cols]) + _f32(both.astype(jnp.bfloat16))).astype(jnp.bfloat16)
            y_start(i, slot, cols)
        y_local(i, slot).start()

        @pl.when(i < eager)
        def _():
            y_mate(i, slot).start()

            @pl.when(i >= 1)
            def _():
                y_forward(i - 1)

    def step(i, carry):
        def attention_kind(kind, inner):
            attention(kind, i)
            return inner

        lax.fori_loop(0, 2, attention_kind, 0)

        @pl.when(lagged & (i >= 1))
        def _():
            finish(i - 1)
        mlp(MATE, i)
        mlp(OWN, i)

        @pl.when(jnp.logical_not(lagged))
        def _():
            finish(i)
        return carry

    lax.fori_loop(0, units, step, 0)

    @pl.when(lagged)
    def _():
        finish(units - 1)

    for i in range(max(units - 2, 0), units):
        y_wait(i, i % 2)

    def late(i, carry):
        y_mate_late(i).start()
        return carry

    def forward(i, carry):
        y_forward(i)
        return carry

    lax.fori_loop(eager, units, late, 0)
    lax.fori_loop(jnp.maximum(eager - 1, 0), units, forward, 0)

    for i in range(max(units - 2, 0), units):
        for kind in range(2):
            for grp in range(2):
                o_copy(kind, i % 2, grp).wait_send()

        @pl.when(has_prev)
        def _():
            wb_copy(i, i % 2).wait_send()
    for idx in range(p_chunks):
        p_copy(0, idx).wait_send()
    for copy in passes:
        copy.wait_send()

    @pl.when(jnp.logical_not(lender) & lends_all)
    def _():
        remote(relay_a, relay_b, hop_sem.at[0], rb_sem.at[0], to_mate).wait_send()
        remote(relay_b, wdn.at[1], hop_sem.at[1], wr_sem.at[7], {"pp": ally}).wait_send()

    @pl.when(jnp.logical_not(lender) & jnp.logical_not(lends_all))
    def _():
        some = pl.ds(0, lend_some * part)
        remote(relay_a.at[some], relay_b.at[some], hop_sem.at[0], rb_sem.at[0], to_mate).wait_send()
        remote(relay_b.at[some], wdn.at[1, some], hop_sem.at[1], wr_sem.at[7], {"pp": ally}).wait_send()

    def late_sent(i, carry):
        y_mate_late(i).wait_send()
        return carry

    lax.fori_loop(eager, units, late_sent, 0)

    def arrived(i, carry):
        by_mate = is_last & (i % 2 == 0)

        @pl.when(by_mate)
        def _():
            y_mate_late(i).wait_recv()

        @pl.when(jnp.logical_not(by_mate))
        def _():
            twin_arrival(i).wait_recv()
        return carry

    lax.fori_loop(0, units, arrived, 0)
    mate_rows = pl.ds(mate * units, units)
    remote(y_hbm.at[mate_rows], y_hbm.at[mate_rows], yf_sem.at[0], yf_sem.at[1], to_twin).wait()


def solution(mesh):
    stages = mesh.shape["pp"]
    weight_specs = (
        P('pp', None), P('pp', None),
        P('pp', None, None, 'tp', None), P('pp', None, 'tp', None),
        P('pp', 'tp', None, None), P('pp', None),
        P('pp', None), P('pp', None),
        P('pp', None, 'tp'), P('pp', 'tp'),
        P('pp', 'tp', None), P('pp', None),
    )
    if mesh.shape["tp"] != 4 or stages % 4:
        raise ValueError("unsupported mesh")

    def local_run(x_micro, ln1_gain, ln1_bias, w_qkv, b_qkv, w_out, b_out, ln2_gain, ln2_bias, w_up, b_up, w_down, b_down):
        micro, rows, seq, d_model = x_micro.shape
        total = micro * rows
        units = total // mesh.shape["tp"]
        _, _, _, heads, head_dim = w_qkv.shape
        group_w = heads * head_dim
        ff = w_up.shape[-1]
        x_seqs = x_micro.reshape(total, seq, d_model)
        w_qkv = jnp.transpose(w_qkv[0], (0, 2, 3, 1)).reshape(3 * group_w, d_model)
        w_out = w_out.reshape(group_w, d_model)
        any_spec = pl.BlockSpec(memory_space=pl.ANY)
        vmem_spec = pl.BlockSpec(memory_space=pltpu.VMEM)
        bf16, dma = jnp.bfloat16, pltpu.SemaphoreType.DMA
        p_chunks = d_model // DOWN_CHUNK
        y_all = pl.pallas_call(
            functools.partial(_pipeline_kernel, stages, head_dim),
            out_shape=jax.ShapeDtypeStruct((total, seq, d_model), bf16),
            in_specs=[any_spec] * 5 + [vmem_spec, any_spec] + [vmem_spec] * 6,
            out_specs=any_spec,
            scratch_shapes=[
                pltpu.VMEM((d_model, 6 * group_w), bf16),
                pltpu.VMEM((4, group_w, d_model), bf16),
                pltpu.VMEM((2, d_model, ff), bf16),
                pltpu.VMEM((2, ff, d_model), bf16),
                pltpu.VMEM((1, 6 * group_w), jnp.float32),
                pltpu.VMEM((2, 1, ff), bf16),
                pltpu.VMEM((2, units, seq, d_model), bf16),
                pltpu.VMEM((seq, d_model), bf16),
                pltpu.VMEM((seq, 6 * group_w), bf16),
                pltpu.VMEM((2, 2, 2, seq, 2 * group_w), bf16),
                pltpu.VMEM((seq, d_model), jnp.float32),
                pltpu.VMEM((seq, d_model), bf16),
                pltpu.VMEM((2, seq, ff), bf16),
                pltpu.VMEM((2, seq, d_model), bf16),
                pltpu.VMEM((2, seq, d_model), bf16),
                pltpu.VMEM((2, seq, d_model), bf16),
                pltpu.VMEM((ff, d_model), bf16),
                pltpu.VMEM((ff, d_model), bf16),
                pltpu.VMEM((2, TURN_ROWS, d_model), bf16),
                dma((2, units)), dma((6,)), dma((10,)), dma((10,)),
                dma((2, 2, 2)), dma((2, 2, 2)), dma((p_chunks,)), dma((2, p_chunks)),
                dma((2,)), dma((2,)), dma((2,)), dma((2,)), dma((units,)), dma((2,)), dma((units,)), dma((units,)),
                dma((2,)), dma((RELAY_STEPS,)), dma((RELAY_STEPS,)), dma((2,)),
            ],
            compiler_params=pltpu.CompilerParams(collective_id=0, has_side_effects=True, vmem_limit_bytes=60 * 1024 * 1024),
            name="stage_pipeline",
        )(x_seqs, w_qkv, w_out, w_up.reshape(d_model, ff), w_down.reshape(ff, d_model), b_qkv, b_up,
          ln1_gain, ln1_bias, b_out, ln2_gain, ln2_bias, b_down)
        return y_all.reshape(1, micro, rows, seq, d_model)

    return jax.shard_map(local_run, mesh=mesh, in_specs=(P(None, 'dp', None, None),) + weight_specs, out_specs=P('pp', None, 'dp', None, None), check_vma=False)
```

time: 634 us -> 600 us (0.946)
  Pallas kernels: 610 us -> 582 us
  local copies, waits for them, and re-layouts: 23.9 us -> 16.9 us
    pallas_call x1, Pallas kernels: 610 us -> 582 us  [local_run(): pl.pallas_call(functools.partial(_pipeline_kernel, stages, head_dim), out...]
    reshape x2 -> x0, local copies, waits for them, and re-layouts: 7.07 us -> none  [the longest x1 5.72 us: local_run(): w_qkv = jnp.transpose(w_qkv[0], (1, 0, 2, 3)).reshape(d_model, 3 * group_w)]
where the time goes in v3:
time: 600 us; the launch traced here: 599 us
  Pallas kernels  582 us (97%)
  local copies, waits for them, and re-layouts  16.9 us (3%)
    pallas_call x1, Pallas kernels, local_run(): pl.pallas_call(functools.partial(_pipeline_kernel, stages, head_dim), out...  582 us
    unnamed x1, local copies, waits for them, and re-layouts  16.9 us

profile of v3, /device:TPU:103, one launch (start us, length us, event | category | flops | bytes accessed | tf_op | source)
XLA Modules:
  0.0 599.2 jit_solution(7262234177326703603)
XLA Ops:
  0.0 582.4 %stage_pipeline.1 = bf16[48,128,1536]{2,1,0:T(8,128)(2,1)} custom-call(bf16[48,128,1536]{2,1,0:T(8,128)(2,1)} %bitcast.11, bf16[1152,1536]{1,0:T(8,128)(2,1)} %bitcast.14, bf16[384,1536]{1,0:T(8,128)(2,1)} %bitcast.15, bf16[1536,1536]{1,0:T(8,128)(2,1)} %bitcast.12, bf16[1536,1536]{1,0:T(8,128)(2,1)} %bitcast.13, bf16[1,3,4,96]{3,2,1,0:T(4,128)(2,1)} %bqkv_in.1, ...), custom_call_target="tpu_custom_call" | custom-call | tf_op jit(solution)/shard_map/stage_pipeline/pallas_call | solution.py:572
  582.4 16.9 %copy.15 = bf16[1,8,6,128,1536]{4,3,2,1,0:T(8,128)(2,1)} copy(bf16[1,8,6,128,1536]{4,3,2,1,0:T(8,128)(2,1)} %bitcast.10) | data formatting | bytes 37748736

commit v4 on v3

--- a/solution.py
+++ b/solution.py
@@ -8,6 +8,7 @@
 from jax.sharding import PartitionSpec as P
 
 LN_EPS = 1e-5
+LOG2_E = 1.4426950408889634
 MESH = pl.DeviceIdType.MESH
 LN_ROWS = 16
 UP_CHUNK = 512
@@ -15,8 +16,11 @@
 OUT_CHUNK = 512
 RELAY_STEPS = 16
 LAGGED_STAGES = 2
-EAGER_UNITS = (0, 0, 1, 12)
+RELAY_UNITS = 10
+EAGER_UNITS = (0, 0, 2, 12)
 TURN_ROWS = 128
+COPY_ROWS = 4
+COPY_SLOTS = 8
 
 
 def _f32(val):
@@ -41,12 +45,12 @@
                      wqkv, wout, wup, wdn, bqkv, bup, xbuf, hbuf, qkv, obuf, acc, x1buf, ubuf, pown, prcv, ybuf,
                      relay_a, relay_b, turn,
                      x_sem, wl_sem, ws_sem, wr_sem, os_sem, or_sem, ps_sem, pr_sem, yl_sem, yn_sem, yd_sem, ym_sem, ymr_sem, yf_sem, yt_sem, yl_late,
-                     wb_sem, ra_sem, rb_sem, hop_sem):
+                     wb_sem, ra_sem, rb_sem, hop_sem, rya_sem, ryb_sem, ryh_sem):
     _, units, seq, d_model = xbuf.shape
     group_w = wout_hbm.shape[0]
     group_heads = group_w // head_dim
     qk_w = 2 * group_w
-    v_col = 2 * qk_w
+    v_col, twin_col = qk_w, qk_w + 2 * group_w
     ff = wup_hbm.shape[1]
     rr = lax.axis_index("tp")
     pp = lax.axis_index("pp")
@@ -58,6 +62,9 @@
     has_prev = pp > 0
     lagged = pp >= stages - LAGGED_STAGES
     is_last = pp == stages - 1
+    relayed = jnp.where(pp >= stages - stages // 4, min(RELAY_UNITS, units), 0)
+    helps = pp < stages // 4
+    cross = rr + 2 - 4 * (rr // 2)
     eager = 0
     for quarter, amount in enumerate(EAGER_UNITS):
         eager = eager + jnp.where(pp * len(EAGER_UNITS) // stages == quarter, min(amount, units), 0)
@@ -71,7 +78,26 @@
     def remote(src, dst, send, recv, dev):
         return pltpu.make_async_remote_copy(src_ref=src, dst_ref=dst, send_sem=send, recv_sem=recv, device_id=dev, device_id_type=MESH)
 
-    own_qk, twin_qk = pl.ds(0, qk_w), pl.ds(qk_w, qk_w)
+    barrier = pltpu.get_barrier_semaphore()
+
+    def greet(dev):
+        pl.semaphore_signal(barrier, inc=1, device_id=dev, device_id_type=MESH)
+
+    greet({"tp": mate})
+    greet({"tp": twin})
+    greet({"pp": ally})
+
+    @pl.when(has_next)
+    def _():
+        greet({"pp": pp + 1})
+        greet({"tp": twin, "pp": pp + 1})
+
+    @pl.when(has_prev)
+    def _():
+        greet({"pp": pp - 1})
+        greet({"tp": mate, "pp": pp - 1})
+
+    own_qk, twin_qk = pl.ds(0, qk_w), pl.ds(twin_col, qk_w)
     own_v, twin_v = pl.ds(v_col, group_w), pl.ds(v_col + group_w, group_w)
     turn_rows = turn.shape[1]
     turns = 3 * group_w // turn_rows
@@ -116,25 +142,6 @@
     for copy in loads:
         copy.start()
 
-    barrier = pltpu.get_barrier_semaphore()
-
-    def greet(dev):
-        pl.semaphore_signal(barrier, inc=1, device_id=dev, device_id_type=MESH)
-
-    greet(to_mate)
-    greet(to_twin)
-    greet({"pp": ally})
-
-    @pl.when(has_next)
-    def _():
-        greet({"pp": pp + 1})
-        greet({"tp": twin, "pp": pp + 1})
-
-    @pl.when(has_prev)
-    def _():
-        greet({"pp": pp - 1})
-        greet({"tp": mate, "pp": pp - 1})
-
     pl.semaphore_wait(barrier, 3 + 2 * (jnp.where(has_next, 1, 0) + jnp.where(has_prev, 1, 0)))
 
     passes[2].start()
@@ -173,9 +180,7 @@
     def turn_block(c, carry):
         slot = c % 2
         turn_load(c, slot).wait()
-        first = c * turn_rows
-        col = first + (first // qk_w) * (v_col - qk_w)
-        wqkv[:, pl.ds(pl.multiple_of(col, 128), turn_rows)] = turn[slot].T
+        wqkv[:, pl.ds(pl.multiple_of(c * turn_rows, 128), turn_rows)] = turn[slot].T
 
         @pl.when(c + 2 < turns)
         def _():
@@ -194,8 +199,7 @@
     in_head = (head_lane >= head_row * head_dim) & (head_lane < (head_row + 1) * head_dim)
     for third in range(3):
         wide = jnp.where(in_head, _dot(bqkv_in[0, third], spread), 0.0)
-        col = third * group_w if third < 2 else v_col
-        bqkv[:, pl.ds(col, group_w)] = jnp.sum(wide, axis=0, keepdims=True)
+        bqkv[:, pl.ds(third * group_w, group_w)] = jnp.sum(wide, axis=0, keepdims=True)
     for idx in (0, 8, 1, 9, 5, 6):
         passes[idx].start()
 
@@ -278,18 +282,36 @@
         ref = y_hbm.at[twin * units + i]
         return remote(ref, ref, yd_sem.at[0], yt_sem.at[i], to_twin)
 
+    def y_hop_in(i):
+        return remote(y_hbm.at[mate * units + i], relay_a.at[pl.ds(i * seq, seq)], yf_sem.at[0], rya_sem.at[i], {"pp": ally})
+
+    def y_hop_over(i):
+        rows = pl.ds(i * seq, seq)
+        return remote(relay_a.at[rows], relay_b.at[rows], ryh_sem.at[0], ryb_sem.at[i], to_mate)
+
+    def y_hop_out(i):
+        return remote(relay_b.at[pl.ds(i * seq, seq)], y_hbm.at[cross * units + i], ryh_sem.at[1], yf_sem.at[1], {"pp": ally})
+
+    def by_mate(i):
+        return is_last & (i % 2 == 0) & (i >= relayed)
+
     def y_forward(i):
-        by_mate = is_last & (i % 2 == 0)
-
-        @pl.when(by_mate)
+        @pl.when(by_mate(i))
         def _():
             twin_arrival(i).wait_recv()
             y_forward_twin(i).start()
 
-        @pl.when(jnp.logical_not(by_mate))
+        @pl.when(jnp.logical_not(by_mate(i)))
         def _():
             y_mate_late(i).wait_recv()
-            y_forward_mate(i).start()
+
+            @pl.when(i < relayed)
+            def _():
+                y_hop_in(i).start()
+
+            @pl.when(i >= relayed)
+            def _():
+                y_forward_mate(i).start()
 
     def y_start(i, slot, cols):
         @pl.when(has_next)
@@ -358,29 +380,31 @@
             return jnp.concatenate([jnp.where(m, act, zero) for m in masks], axis=0)
 
         def scores_of(grp):
-            q_heads = by_head(qkv[:, pl.ds(grp * qk_w, group_w)])
-            key = qkv[:, pl.ds(grp * qk_w + group_w, group_w)]
+            q_heads = by_head(qkv[:, pl.ds(grp * twin_col, group_w)])
+            key = qkv[:, pl.ds(grp * twin_col + group_w, group_w)]
             return lax.dot_general(q_heads, key, (((1,), (1,)), ((), ())), preferred_element_type=jnp.float32)
 
         def probs_of(scores):
             probs = []
             for hd in range(group_heads):
-                sc = jnp.where(causal, scores[hd * seq:(hd + 1) * seq] * (head_dim ** -0.5), -1e30)
-                ex = jnp.exp(sc - jnp.max(sc, axis=-1, keepdims=True))
+                sc = jnp.where(causal, scores[hd * seq:(hd + 1) * seq], -1e30)
+                ex = jnp.exp2((sc - jnp.max(sc, axis=-1, keepdims=True)) * (head_dim ** -0.5 * LOG2_E))
                 probs.append((ex * (1.0 / jnp.sum(ex, axis=-1, keepdims=True))).astype(jnp.bfloat16))
             return jnp.concatenate(probs, axis=1)
 
+        def send_heads(grp, probs):
+            val = qkv[:, pl.ds(v_col + grp * group_w, group_w)]
+            obuf[slot, kind, 0, :, pl.ds(grp * group_w, group_w)] = _dot(probs, by_head(val)).astype(jnp.bfloat16)
+            o_copy(kind, slot, grp).start()
+
         project(0)
         scores_0 = scores_of(0)
-        project(qk_w)
+        project(twin_col)
         probs_0 = probs_of(scores_0)
         scores_1 = scores_of(1)
         project(v_col)
-        probs_1 = probs_of(scores_1)
-        for grp, probs in enumerate((probs_0, probs_1)):
-            val = qkv[:, pl.ds(v_col + grp * group_w, group_w)]
-            obuf[slot, kind, 0, :, pl.ds(grp * group_w, group_w)] = _dot(probs, by_head(val)).astype(jnp.bfloat16)
-            o_copy(kind, slot, grp).start()
+        send_heads(0, probs_0)
+        send_heads(1, probs_of(scores_1))
 
     def mlp(kind, i):
         slot = i % 2
@@ -389,17 +413,19 @@
             def _():
                 wait_weights((0,), (3, 4))
 
-        def out_part(half, cols):
+        def out_part(half, cols, kind=kind):
             return _dot(obuf[slot, kind, half], jnp.concatenate([wout[2 * half, :, cols], wout[2 * half + 1, :, cols]], axis=0))
 
-        for c0 in range(0, d_model, OUT_CHUNK):
-            cols = pl.ds(c0, OUT_CHUNK)
-            acc[:, cols] = out_part(0, cols)
+        if kind == MATE:
+            for both in (MATE, OWN):
+                for c0 in range(0, d_model, OUT_CHUNK):
+                    cols = pl.ds(c0, OUT_CHUNK)
+                    acc[both, :, cols] = out_part(0, cols, both)
         for grp in range(2):
             o_copy(1 - kind, slot, grp).wait_recv()
         for c0 in range(0, d_model, OUT_CHUNK):
             cols = pl.ds(c0, OUT_CHUNK)
-            att = ((acc[:, cols] + out_part(1, cols)) + _f32(b_out[:, cols])).astype(jnp.bfloat16)
+            att = ((acc[kind, :, cols] + out_part(1, cols)) + _f32(b_out[:, cols])).astype(jnp.bfloat16)
             x1buf[:, cols] = (_f32(xbuf[kind, i, :, cols]) + _f32(att)).astype(jnp.bfloat16)
 
         gain, bias = _f32(ln2_gain[...]), _f32(ln2_bias[...])
@@ -495,6 +521,27 @@
     lax.fori_loop(eager, units, late, 0)
     lax.fori_loop(jnp.maximum(eager - 1, 0), units, forward, 0)
 
+    helped = min(RELAY_UNITS, units)
+
+    @pl.when(helps)
+    def _():
+        def pass_on(i, carry):
+            @pl.when(i < helped)
+            def _():
+                y_hop_in(i).wait_recv()
+                y_hop_over(i).start()
+
+            @pl.when(i >= 1)
+            def _():
+                y_hop_over(i - 1).wait_recv()
+                y_hop_out(i - 1).start()
+            return carry
+
+        lax.fori_loop(0, helped + 1, pass_on, 0)
+        rows = pl.ds(0, helped * seq)
+        remote(relay_a.at[rows], relay_b.at[rows], ryh_sem.at[0], ryb_sem.at[0], to_mate).wait_send()
+        remote(relay_b.at[rows], relay_a.at[rows], ryh_sem.at[1], yf_sem.at[1], {"pp": ally}).wait_send()
+
     for i in range(max(units - 2, 0), units):
         for kind in range(2):
             for grp in range(2):
@@ -526,13 +573,11 @@
     lax.fori_loop(eager, units, late_sent, 0)
 
     def arrived(i, carry):
-        by_mate = is_last & (i % 2 == 0)
-
-        @pl.when(by_mate)
+        @pl.when(by_mate(i))
         def _():
             y_mate_late(i).wait_recv()
 
-        @pl.when(jnp.logical_not(by_mate))
+        @pl.when(jnp.logical_not(by_mate(i)))
         def _():
             twin_arrival(i).wait_recv()
         return carry
@@ -540,6 +585,28 @@
     lax.fori_loop(0, units, arrived, 0)
     mate_rows = pl.ds(mate * units, units)
     remote(y_hbm.at[mate_rows], y_hbm.at[mate_rows], yf_sem.at[0], yf_sem.at[1], to_twin).wait()
+
+
+def _copy_kernel(src, dst, buf, in_sem, out_sem):
+    slots, rows = buf.shape[:2]
+    blocks = src.shape[0] // rows
+
+    def load(c):
+        return pltpu.make_async_copy(src.at[pl.ds(c * rows, rows)], buf.at[c % slots], in_sem.at[c % slots])
+
+    def store(c):
+        return pltpu.make_async_copy(buf.at[c % slots], dst.at[pl.ds(c * rows, rows)], out_sem.at[c % slots])
+
+    for c in range(min(slots, blocks)):
+        load(c).start()
+    for c in range(blocks):
+        load(c).wait()
+        store(c).start()
+        if c >= 1 and c - 1 + slots < blocks:
+            store(c - 1).wait()
+            load(c - 1 + slots).start()
+    for c in range(max(blocks - slots, 0), blocks):
+        store(c).wait()
 
 
 def solution(mesh):
@@ -585,7 +652,7 @@
                 pltpu.VMEM((seq, d_model), bf16),
                 pltpu.VMEM((seq, 6 * group_w), bf16),
                 pltpu.VMEM((2, 2, 2, seq, 2 * group_w), bf16),
-                pltpu.VMEM((seq, d_model), jnp.float32),
+                pltpu.VMEM((2, seq, d_model), jnp.float32),
                 pltpu.VMEM((seq, d_model), bf16),
                 pltpu.VMEM((2, seq, ff), bf16),
                 pltpu.VMEM((2, seq, d_model), bf16),
@@ -598,11 +665,22 @@
                 dma((2, 2, 2)), dma((2, 2, 2)), dma((p_chunks,)), dma((2, p_chunks)),
                 dma((2,)), dma((2,)), dma((2,)), dma((2,)), dma((units,)), dma((2,)), dma((units,)), dma((units,)),
                 dma((2,)), dma((RELAY_STEPS,)), dma((RELAY_STEPS,)), dma((2,)),
+                dma((units,)), dma((units,)), dma((2,)),
             ],
             compiler_params=pltpu.CompilerParams(collective_id=0, has_side_effects=True, vmem_limit_bytes=60 * 1024 * 1024),
             name="stage_pipeline",
         )(x_seqs, w_qkv, w_out, w_up.reshape(d_model, ff), w_down.reshape(ff, d_model), b_qkv, b_up,
           ln1_gain, ln1_bias, b_out, ln2_gain, ln2_bias, b_down)
+        block_rows = max(d for d in range(1, COPY_ROWS + 1) if total % d == 0)
+        y_all = pl.pallas_call(
+            _copy_kernel,
+            out_shape=jax.ShapeDtypeStruct((total, seq, d_model), bf16),
+            in_specs=[any_spec],
+            out_specs=any_spec,
+            scratch_shapes=[pltpu.VMEM((COPY_SLOTS, block_rows, seq, d_model), bf16), dma((COPY_SLOTS,)), dma((COPY_SLOTS,))],
+            compiler_params=pltpu.CompilerParams(vmem_limit_bytes=56 * 1024 * 1024),
+            name="result_copy",
+        )(y_all)
         return y_all.reshape(1, micro, rows, seq, d_model)
 
     return jax.shard_map(local_run, mesh=mesh, in_specs=(P(None, 'dp', None, None),) + weight_specs, out_specs=P('pp', None, 'dp', None, None), check_vma=False)

time: 600 us -> 580 us (0.967)
  local copies, waits for them, and re-layouts: 16.9 us -> 0 us
    pallas_call x1, Pallas kernels: 582 us -> 564 us  [local_run(): pl.pallas_call(functools.partial(_pipeline_kernel, stages, head_dim), out...]
    unnamed x1 -> x0, local copies, waits for them, and re-layouts: 16.9 us -> none
    pallas_call x0 -> x1, Pallas kernels: none -> 13.4 us  [local_run(): pl.pallas_call(_copy_kernel, out_shape=jax.ShapeDtypeStruct((total, seq,...]
where the time goes in v4:
time: 580 us; the launch traced here: 577 us
  Pallas kernels  577 us (99%)
    pallas_call x1, Pallas kernels, local_run(): pl.pallas_call(functools.partial(_pipeline_kernel, stages, head_dim), out...  564 us
    pallas_call x1, Pallas kernels, local_run(): pl.pallas_call(_copy_kernel, out_shape=jax.ShapeDtypeStruct((total, seq,...  13.4 us

profile of v4, /device:TPU:103, one launch (start us, length us, event | category | flops | bytes accessed | tf_op | source)
XLA Modules:
  0.0 576.9 jit_solution(10650774909843034524)
XLA Ops:
  0.0 563.5 %stage_pipeline.1.src = bf16[48,128,1536]{2,1,0:T(8,128)(2,1)} custom-call(bf16[48,128,1536]{2,1,0:T(8,128)(2,1)} %bitcast.10, bf16[1152,1536]{1,0:T(8,128)(2,1)} %bitcast.13, bf16[384,1536]{1,0:T(8,128)(2,1)} %bitcast.14, bf16[1536,1536]{1,0:T(8,128)(2,1)} %bitcast.11, bf16[1536,1536]{1,0:T(8,128)(2,1)} %bitcast.12, bf16[1,3,4,96]{3,2,1,0:T(4,128)(2,1)} %bqkv_in.1, ...), custom_call_target="tpu_custom_call" | custom-call | tf_op jit(solution)/shard_map/stage_pipeline/pallas_call | solution.py:639
  563.5 13.4 %result_copy.1 = bf16[48,128,1536]{2,1,0:T(8,128)(2,1)} custom-call(bf16[48,128,1536]{2,1,0:T(8,128)(2,1)} %stage_pipeline.1.src), custom_call_target="tpu_custom_call" | custom-call | tf_op jit(solution)/shard_map/result_copy/pallas_call | solution.py:675

commit v5 on v4

--- a/solution.py
+++ b/solution.py
@@ -16,11 +16,13 @@
 OUT_CHUNK = 512
 RELAY_STEPS = 16
 LAGGED_STAGES = 2
-RELAY_UNITS = 10
+LAG_PLACES = (1, 1)
+COPY_PLACES = (0, 0)
+RELAY_UNITS = (0, 0, 0, 10)
 EAGER_UNITS = (0, 0, 2, 12)
 TURN_ROWS = 128
-COPY_ROWS = 4
-COPY_SLOTS = 8
+COPY_ROWS = 1
+COPY_SLOTS = 32
 
 
 def _f32(val):
@@ -39,13 +41,14 @@
     return jnp.dot(lhs, rhs, preferred_element_type=jnp.float32)
 
 
-def _pipeline_kernel(stages, head_dim, x_hbm, wqkv_hbm, wout_hbm, wup_hbm, wdn_hbm, bqkv_in, bup_in,
-                     ln1_gain, ln1_bias, b_out, ln2_gain, ln2_bias, b_down,
+def _pipeline_kernel(stages, head_dim, x_hbm, wqkv_hbm, wout_hbm, wup_hbm, wdn_hbm, bqkv_hbm, bup_in,
+                     ln1_gain_hbm, ln1_bias_hbm, b_out_hbm, ln2_gain_hbm, ln2_bias_hbm, b_down_hbm,
                      y_hbm,
                      wqkv, wout, wup, wdn, bqkv, bup, xbuf, hbuf, qkv, obuf, acc, x1buf, ubuf, pown, prcv, ybuf,
                      relay_a, relay_b, turn,
                      x_sem, wl_sem, ws_sem, wr_sem, os_sem, or_sem, ps_sem, pr_sem, yl_sem, yn_sem, yd_sem, ym_sem, ymr_sem, yf_sem, yt_sem, yl_late,
-                     wb_sem, ra_sem, rb_sem, hop_sem, rya_sem, ryb_sem, ryh_sem):
+                     wb_sem, ra_sem, rb_sem, hop_sem, rya_sem, ryb_sem, ryh_sem,
+                     bqkv_in, ln1_gain, ln1_bias, b_out, ln2_gain, ln2_bias, b_down, small_sem):
     _, units, seq, d_model = xbuf.shape
     group_w = wout_hbm.shape[0]
     group_heads = group_w // head_dim
@@ -62,12 +65,17 @@
     has_prev = pp > 0
     lagged = pp >= stages - LAGGED_STAGES
     is_last = pp == stages - 1
-    relayed = jnp.where(pp >= stages - stages // 4, min(RELAY_UNITS, units), 0)
-    helps = pp < stages // 4
+    copy_place = jnp.where(is_last, COPY_PLACES[1], COPY_PLACES[0])
+    lag_place = jnp.where(is_last, LAG_PLACES[1], LAG_PLACES[0])
     cross = rr + 2 - 4 * (rr // 2)
-    eager = 0
-    for quarter, amount in enumerate(EAGER_UNITS):
-        eager = eager + jnp.where(pp * len(EAGER_UNITS) // stages == quarter, min(amount, units), 0)
+    quarter = pp * 4 // stages
+
+    def by_quarter(amounts, at):
+        return sum(jnp.where(at == idx, min(amount, units), 0) for idx, amount in enumerate(amounts))
+
+    eager = by_quarter(EAGER_UNITS, quarter)
+    relayed = by_quarter(RELAY_UNITS, quarter)
+    helped = by_quarter(RELAY_UNITS, 3 - quarter)
     lender = pp < stages // 2
     ally = stages - 1 - pp
     OWN, MATE = 0, 1
@@ -128,6 +136,14 @@
     def x_load(kind, i, row):
         return local(x_hbm.at[row * units + i], xbuf.at[kind, i], x_sem.at[kind, i])
 
+    small = [
+        local(src, dst, small_sem.at[idx])
+        for idx, (src, dst) in enumerate([
+            (bqkv_hbm, bqkv_in), (ln1_gain_hbm, ln1_gain), (ln1_bias_hbm, ln1_bias), (b_out_hbm, b_out),
+            (ln2_gain_hbm, ln2_gain), (ln2_bias_hbm, ln2_bias), (b_down_hbm, b_down)])
+    ]
+    for copy in small:
+        copy.start()
     turn_load(0, 0).start()
     turn_load(1, 1).start()
 
@@ -188,6 +204,8 @@
         return carry
 
     lax.fori_loop(0, turns, turn_block, 0)
+    for copy in small:
+        copy.wait()
     spread_row = lax.broadcasted_iota(jnp.int32, (head_dim, group_w), 0)
     spread_col = lax.broadcasted_iota(jnp.int32, (head_dim, group_w), 1)
     spread = jnp.zeros((head_dim, group_w), jnp.float32)
@@ -369,7 +387,7 @@
 
         lane_head = lax.broadcasted_iota(jnp.int32, (seq, group_w), 1)
         masks = [(lane_head >= hd * head_dim) & (lane_head < (hd + 1) * head_dim) for hd in range(group_heads)]
-        causal = row_id >= col_id
+        causal = row_id <= col_id
 
         def project(col):
             cols = pl.ds(col, qk_w)
@@ -382,14 +400,14 @@
         def scores_of(grp):
             q_heads = by_head(qkv[:, pl.ds(grp * twin_col, group_w)])
             key = qkv[:, pl.ds(grp * twin_col + group_w, group_w)]
-            return lax.dot_general(q_heads, key, (((1,), (1,)), ((), ())), preferred_element_type=jnp.float32)
+            return lax.dot_general(key, q_heads, (((1,), (1,)), ((), ())), preferred_element_type=jnp.float32)
 
         def probs_of(scores):
             probs = []
             for hd in range(group_heads):
-                sc = jnp.where(causal, scores[hd * seq:(hd + 1) * seq], -1e30)
-                ex = jnp.exp2((sc - jnp.max(sc, axis=-1, keepdims=True)) * (head_dim ** -0.5 * LOG2_E))
-                probs.append((ex * (1.0 / jnp.sum(ex, axis=-1, keepdims=True))).astype(jnp.bfloat16))
+                sc = jnp.where(causal, scores[:, hd * seq:(hd + 1) * seq], -1e30)
+                ex = jnp.exp2((sc - jnp.max(sc, axis=0, keepdims=True)) * (head_dim ** -0.5 * LOG2_E))
+                probs.append((ex * (1.0 / jnp.sum(ex, axis=0, keepdims=True))).astype(jnp.bfloat16).T)
             return jnp.concatenate(probs, axis=1)
 
         def send_heads(grp, probs):
@@ -399,12 +417,10 @@
 
         project(0)
         scores_0 = scores_of(0)
+        project(v_col)
+        send_heads(0, probs_of(scores_0))
         project(twin_col)
-        probs_0 = probs_of(scores_0)
-        scores_1 = scores_of(1)
-        project(v_col)
-        send_heads(0, probs_0)
-        send_heads(1, probs_of(scores_1))
+        send_heads(1, probs_of(scores_of(1)))
 
     def mlp(kind, i):
         slot = i % 2
@@ -426,12 +442,12 @@
         for c0 in range(0, d_model, OUT_CHUNK):
             cols = pl.ds(c0, OUT_CHUNK)
             att = ((acc[kind, :, cols] + out_part(1, cols)) + _f32(b_out[:, cols])).astype(jnp.bfloat16)
-            x1buf[:, cols] = (_f32(xbuf[kind, i, :, cols]) + _f32(att)).astype(jnp.bfloat16)
+            x1buf[kind, :, cols] = (_f32(xbuf[kind, i, :, cols]) + _f32(att)).astype(jnp.bfloat16)
 
         gain, bias = _f32(ln2_gain[...]), _f32(ln2_bias[...])
         for r0 in range(0, seq, LN_ROWS):
             rows = pl.ds(r0, LN_ROWS)
-            hbuf[rows, :] = _norm_rows(_f32(x1buf[rows, :]), gain, bias)
+            hbuf[rows, :] = _norm_rows(_f32(x1buf[kind, rows, :]), gain, bias)
 
         if kind == MATE:
             @pl.when(i == 0)
@@ -471,34 +487,54 @@
             cols = pl.ds(idx * DOWN_CHUNK, DOWN_CHUNK)
             p_copy(slot, idx).wait_recv()
             both = (_f32(pown[OWN, :, cols]) + _f32(prcv[slot, :, cols])) + _f32(b_down[:, cols])
-            ybuf[slot, :, cols] = (_f32(x1buf[:, cols]) + _f32(both.astype(jnp.bfloat16))).astype(jnp.bfloat16)
+            ybuf[slot, :, cols] = (_f32(x1buf[OWN, :, cols]) + _f32(both.astype(jnp.bfloat16))).astype(jnp.bfloat16)
             y_start(i, slot, cols)
         y_local(i, slot).start()
 
+    def replicate(i):
         @pl.when(i < eager)
         def _():
-            y_mate(i, slot).start()
+            y_mate(i, i % 2).start()
 
             @pl.when(i >= 1)
             def _():
                 y_forward(i - 1)
 
     def step(i, carry):
+        def finish_before(place):
+            @pl.when(lagged & (i >= 1) & (lag_place == place))
+            def _():
+                finish(i - 1)
+
         def attention_kind(kind, inner):
             attention(kind, i)
+
+            @pl.when(kind == OWN)
+            def _():
+                finish_before(0)
             return inner
 
         lax.fori_loop(0, 2, attention_kind, 0)
-
-        @pl.when(lagged & (i >= 1))
-        def _():
-            finish(i - 1)
+        finish_before(1)
+
+        @pl.when(lagged & (i >= 1) & (copy_place == 0))
+        def _():
+            replicate(i - 1)
         mlp(MATE, i)
+
+        @pl.when(lagged & (i >= 1) & (copy_place == 1))
+        def _():
+            replicate(i - 1)
         mlp(OWN, i)
 
+        @pl.when(lagged & (i >= 1) & (copy_place == 2))
+        def _():
+            replicate(i - 1)
+
         @pl.when(jnp.logical_not(lagged))
         def _():
             finish(i)
+            replicate(i)
         return carry
 
     lax.fori_loop(0, units, step, 0)
@@ -506,6 +542,7 @@
     @pl.when(lagged)
     def _():
         finish(units - 1)
+        replicate(units - 1)
 
     for i in range(max(units - 2, 0), units):
         y_wait(i, i % 2)
@@ -521,9 +558,7 @@
     lax.fori_loop(eager, units, late, 0)
     lax.fori_loop(jnp.maximum(eager - 1, 0), units, forward, 0)
 
-    helped = min(RELAY_UNITS, units)
-
-    @pl.when(helps)
+    @pl.when(helped > 0)
     def _():
         def pass_on(i, carry):
             @pl.when(i < helped)
@@ -538,9 +573,14 @@
             return carry
 
         lax.fori_loop(0, helped + 1, pass_on, 0)
-        rows = pl.ds(0, helped * seq)
-        remote(relay_a.at[rows], relay_b.at[rows], ryh_sem.at[0], ryb_sem.at[0], to_mate).wait_send()
-        remote(relay_b.at[rows], relay_a.at[rows], ryh_sem.at[1], yf_sem.at[1], {"pp": ally}).wait_send()
+
+    for idx, amount in enumerate(RELAY_UNITS):
+        if amount:
+            @pl.when(3 - quarter == idx)
+            def _(amount=amount):
+                rows = pl.ds(0, min(amount, units) * seq)
+                remote(relay_a.at[rows], relay_b.at[rows], ryh_sem.at[0], ryb_sem.at[0], to_mate).wait_send()
+                remote(relay_b.at[rows], relay_a.at[rows], ryh_sem.at[1], yf_sem.at[1], {"pp": ally}).wait_send()
 
     for i in range(max(units - 2, 0), units):
         for kind in range(2):
@@ -633,13 +673,12 @@
         w_qkv = jnp.transpose(w_qkv[0], (0, 2, 3, 1)).reshape(3 * group_w, d_model)
         w_out = w_out.reshape(group_w, d_model)
         any_spec = pl.BlockSpec(memory_space=pl.ANY)
-        vmem_spec = pl.BlockSpec(memory_space=pltpu.VMEM)
         bf16, dma = jnp.bfloat16, pltpu.SemaphoreType.DMA
         p_chunks = d_model // DOWN_CHUNK
         y_all = pl.pallas_call(
             functools.partial(_pipeline_kernel, stages, head_dim),
             out_shape=jax.ShapeDtypeStruct((total, seq, d_model), bf16),
-            in_specs=[any_spec] * 5 + [vmem_spec, any_spec] + [vmem_spec] * 6,
+            in_specs=[any_spec] * 13,
             out_specs=any_spec,
             scratch_shapes=[
                 pltpu.VMEM((d_model, 6 * group_w), bf16),
@@ -653,7 +692,7 @@
                 pltpu.VMEM((seq, 6 * group_w), bf16),
                 pltpu.VMEM((2, 2, 2, seq, 2 * group_w), bf16),
                 pltpu.VMEM((2, seq, d_model), jnp.float32),
-                pltpu.VMEM((seq, d_model), bf16),
+                pltpu.VMEM((2, seq, d_model), bf16),
                 pltpu.VMEM((2, seq, ff), bf16),
                 pltpu.VMEM((2, seq, d_model), bf16),
                 pltpu.VMEM((2, seq, d_model), bf16),
@@ -666,6 +705,7 @@
                 dma((2,)), dma((2,)), dma((2,)), dma((2,)), dma((units,)), dma((2,)), dma((units,)), dma((units,)),
                 dma((2,)), dma((RELAY_STEPS,)), dma((RELAY_STEPS,)), dma((2,)),
                 dma((units,)), dma((units,)), dma((2,)),
+                pltpu.VMEM(b_qkv.shape, bf16), *[pltpu.VMEM((1, d_model), bf16) for _ in range(6)], dma((7,)),
             ],
             compiler_params=pltpu.CompilerParams(collective_id=0, has_side_effects=True, vmem_limit_bytes=60 * 1024 * 1024),
             name="stage_pipeline",

time: 580 us -> 573 us (0.988)
  no operation moved by 1% of the time
where the time goes in v5:
time: 573 us
  Pallas kernels  573 us (100%)
    pallas_call x1, Pallas kernels, local_run(): pl.pallas_call(functools.partial(_pipeline_kernel, stages, head_dim), out...  560 us
    pallas_call x1, Pallas kernels, local_run(): pl.pallas_call(_copy_kernel, out_shape=jax.ShapeDtypeStruct((total, seq,...  12.2 us

profile of v5, /device:TPU:103, one launch (start us, length us, event | category | flops | bytes accessed | tf_op | source)
XLA Modules:
  0.0 572.7 jit_solution(12867995328999940050)
XLA Ops:
  0.0 560.5 %stage_pipeline.1.src = bf16[48,128,1536]{2,1,0:T(8,128)(2,1)} custom-call(bf16[48,128,1536]{2,1,0:T(8,128)(2,1)} %bitcast.10, bf16[1152,1536]{1,0:T(8,128)(2,1)} %bitcast.13, bf16[384,1536]{1,0:T(8,128)(2,1)} %bitcast.14, bf16[1536,1536]{1,0:T(8,128)(2,1)} %bitcast.11, bf16[1536,1536]{1,0:T(8,128)(2,1)} %bitcast.12, bf16[1,3,4,96]{3,2,1,0:T(4,128)(2,1)} %bqkv_hbm.1, ...), custom_call_target="tpu_custom_call" | custom-call | tf_op jit(solution)/shard_map/stage_pipeline/pallas_call | solution.py:678
  560.5 12.2 %result_copy.1 = bf16[48,128,1536]{2,1,0:T(8,128)(2,1)} custom-call(bf16[48,128,1536]{2,1,0:T(8,128)(2,1)} %stage_pipeline.1.src), custom_call_target="tpu_custom_call" | custom-call | tf_op jit(solution)/shard_map/result_copy/pallas_call | solution.py:715

commit v6 on v5

--- a/solution.py
+++ b/solution.py
@@ -47,7 +47,7 @@
                      wqkv, wout, wup, wdn, bqkv, bup, xbuf, hbuf, qkv, obuf, acc, x1buf, ubuf, pown, prcv, ybuf,
                      relay_a, relay_b, turn,
                      x_sem, wl_sem, ws_sem, wr_sem, os_sem, or_sem, ps_sem, pr_sem, yl_sem, yn_sem, yd_sem, ym_sem, ymr_sem, yf_sem, yt_sem, yl_late,
-                     wb_sem, ra_sem, rb_sem, hop_sem, rya_sem, ryb_sem, ryh_sem,
+                     wb_sem, ra_sem, rb_sem, hop_sem, rya_sem, ryb_sem, ryh_sem, xo_sem,
                      bqkv_in, ln1_gain, ln1_bias, b_out, ln2_gain, ln2_bias, b_down, small_sem):
     _, units, seq, d_model = xbuf.shape
     group_w = wout_hbm.shape[0]
@@ -65,6 +65,7 @@
     has_prev = pp > 0
     lagged = pp >= stages - LAGGED_STAGES
     is_last = pp == stages - 1
+    hands_over = (odd == 1) & has_next
     copy_place = jnp.where(is_last, COPY_PLACES[1], COPY_PLACES[0])
     lag_place = jnp.where(is_last, LAG_PLACES[1], LAG_PLACES[0])
     cross = rr + 2 - 4 * (rr // 2)
@@ -335,9 +336,12 @@
         @pl.when(has_next)
         def _():
             y_next(i, slot, cols).start()
+
+        @pl.when(odd == 0)
+        def _():
             y_diag(i, slot, cols).start()
 
-        @pl.when(jnp.logical_not(has_next))
+        @pl.when(odd == 1)
         def _():
             y_twin(i, slot, cols).start()
 
@@ -347,15 +351,27 @@
         @pl.when(has_next)
         def _():
             y_next(i, slot, all_cols).wait_send()
+
+        @pl.when(odd == 0)
+        def _():
             y_diag(i, slot, all_cols).wait_send()
 
-        @pl.when(jnp.logical_not(has_next))
+        @pl.when(odd == 1)
         def _():
             y_twin(i, slot, all_cols).wait_send()
 
         @pl.when(i < eager)
         def _():
             y_mate(i, slot).wait_send()
+
+    def x_over(i):
+        return remote(y_hbm.at[twin * units + i], xbuf.at[MATE, i], xo_sem.at[i], x_sem.at[MATE, i], {"pp": pp + 1})
+
+    def hand_over(i):
+        @pl.when(hands_over)
+        def _():
+            twin_arrival(i).wait_recv()
+            x_over(i).start()
 
     def wb_copy(i, slot):
         return remote(xbuf.at[MATE, i], y_hbm.at[mate * units + i], wb_sem.at[slot], yt_sem.at[i], {"pp": pp - 1})
@@ -364,7 +380,7 @@
         slot = i % 2
         x_load(kind, i, rr).wait()
 
-        @pl.when((kind == MATE) & has_prev)
+        @pl.when((kind == MATE) & (odd == 1))
         def _():
             @pl.when(i >= 2)
             def _():
@@ -522,6 +538,10 @@
             replicate(i - 1)
         mlp(MATE, i)
 
+        @pl.when(i >= 1)
+        def _():
+            hand_over(i - 1)
+
         @pl.when(lagged & (i >= 1) & (copy_place == 1))
         def _():
             replicate(i - 1)
@@ -544,6 +564,7 @@
         finish(units - 1)
         replicate(units - 1)
 
+    hand_over(units - 1)
     for i in range(max(units - 2, 0), units):
         y_wait(i, i % 2)
 
@@ -587,7 +608,7 @@
             for grp in range(2):
                 o_copy(kind, i % 2, grp).wait_send()
 
-        @pl.when(has_prev)
+        @pl.when(odd == 1)
         def _():
             wb_copy(i, i % 2).wait_send()
     for idx in range(p_chunks):
@@ -617,9 +638,13 @@
         def _():
             y_mate_late(i).wait_recv()
 
-        @pl.when(jnp.logical_not(by_mate(i)))
+        @pl.when(jnp.logical_not(by_mate(i) | hands_over))
         def _():
             twin_arrival(i).wait_recv()
+
+        @pl.when(hands_over)
+        def _():
+            x_over(i).wait_send()
         return carry
 
     lax.fori_loop(0, units, arrived, 0)
@@ -704,7 +729,7 @@
                 dma((2, 2, 2)), dma((2, 2, 2)), dma((p_chunks,)), dma((2, p_chunks)),
                 dma((2,)), dma((2,)), dma((2,)), dma((2,)), dma((units,)), dma((2,)), dma((units,)), dma((units,)),
                 dma((2,)), dma((RELAY_STEPS,)), dma((RELAY_STEPS,)), dma((2,)),
-                dma((units,)), dma((units,)), dma((2,)),
+                dma((units,)), dma((units,)), dma((2,)), dma((units,)),
                 pltpu.VMEM(b_qkv.shape, bf16), *[pltpu.VMEM((1, d_model), bf16) for _ in range(6)], dma((7,)),
             ],
             compiler_params=pltpu.CompilerParams(collective_id=0, has_side_effects=True, vmem_limit_bytes=60 * 1024 * 1024),

time: 573 us -> 567 us (0.990); the launches traced: 573 us -> 560 us
  Pallas kernels: 573 us -> 560 us
    pallas_call x1, Pallas kernels: 560 us -> 548 us  [local_run(): pl.pallas_call(functools.partial(_pipeline_kernel, stages, head_dim), out...]
where the time goes in v6:
time: 567 us; the launch traced here: 560 us
  Pallas kernels  560 us (99%)
    pallas_call x1, Pallas kernels, local_run(): pl.pallas_call(functools.partial(_pipeline_kernel, stages, head_dim), out...  548 us
    pallas_call x1, Pallas kernels, local_run(): pl.pallas_call(_copy_kernel, out_shape=jax.ShapeDtypeStruct((total, seq,...  12.2 us

profile of v6, /device:TPU:103, one launch (start us, length us, event | category | flops | bytes accessed | tf_op | source)
XLA Modules:
  0.0 560.5 jit_solution(9991498009573195519)
XLA Ops:
  0.0 548.3 %stage_pipeline.1.src = bf16[48,128,1536]{2,1,0:T(8,128)(2,1)} custom-call(bf16[48,128,1536]{2,1,0:T(8,128)(2,1)} %bitcast.10, bf16[1152,1536]{1,0:T(8,128)(2,1)} %bitcast.13, bf16[384,1536]{1,0:T(8,128)(2,1)} %bitcast.14, bf16[1536,1536]{1,0:T(8,128)(2,1)} %bitcast.11, bf16[1536,1536]{1,0:T(8,128)(2,1)} %bitcast.12, bf16[1,3,4,96]{3,2,1,0:T(4,128)(2,1)} %bqkv_hbm.1, ...), custom_call_target="tpu_custom_call" | custom-call | tf_op jit(solution)/shard_map/stage_pipeline/pallas_call | solution.py:703
  548.3 12.2 %result_copy.1 = bf16[48,128,1536]{2,1,0:T(8,128)(2,1)} custom-call(bf16[48,128,1536]{2,1,0:T(8,128)(2,1)} %stage_pipeline.1.src), custom_call_target="tpu_custom_call" | custom-call | tf_op jit(solution)/shard_map/result_copy/pallas_call | solution.py:740

commit v7 on v6

--- a/solution.py
+++ b/solution.py
@@ -18,8 +18,8 @@
 LAGGED_STAGES = 2
 LAG_PLACES = (1, 1)
 COPY_PLACES = (0, 0)
-RELAY_UNITS = (0, 0, 0, 10)
-EAGER_UNITS = (0, 0, 2, 12)
+RELAY_UNITS = (0, 0, 4, 10)
+EAGER_UNITS = (0, 0, 3, 12)
 TURN_ROWS = 128
 COPY_ROWS = 1
 COPY_SLOTS = 32
@@ -531,16 +531,15 @@
             return inner
 
         lax.fori_loop(0, 2, attention_kind, 0)
+        @pl.when(i >= 1)
+        def _():
+            hand_over(i - 1)
         finish_before(1)
 
         @pl.when(lagged & (i >= 1) & (copy_place == 0))
         def _():
             replicate(i - 1)
         mlp(MATE, i)
-
-        @pl.when(i >= 1)
-        def _():
-            hand_over(i - 1)
 
         @pl.when(lagged & (i >= 1) & (copy_place == 1))
         def _():

time: 567 us -> 552 us (0.974)
  Pallas kernels: 560 us -> 551 us
    pallas_call x1, Pallas kernels: 548 us -> 539 us  [local_run(): pl.pallas_call(functools.partial(_pipeline_kernel, stages, head_dim), out...]
where the time goes in v7:
time: 552 us; the launch traced here: 551 us
  Pallas kernels  551 us (100%)
    pallas_call x1, Pallas kernels, local_run(): pl.pallas_call(functools.partial(_pipeline_kernel, stages, head_dim), out...  539 us
    pallas_call x1, Pallas kernels, local_run(): pl.pallas_call(_copy_kernel, out_shape=jax.ShapeDtypeStruct((total, seq,...  12.2 us

profile of v7, /device:TPU:103, one launch (start us, length us, event | category | flops | bytes accessed | tf_op | source)
XLA Modules:
  0.0 551.0 jit_solution(17040681749511483539)
XLA Ops:
  0.0 538.8 %stage_pipeline.1.src = bf16[48,128,1536]{2,1,0:T(8,128)(2,1)} custom-call(bf16[48,128,1536]{2,1,0:T(8,128)(2,1)} %bitcast.10, bf16[1152,1536]{1,0:T(8,128)(2,1)} %bitcast.13, bf16[384,1536]{1,0:T(8,128)(2,1)} %bitcast.14, bf16[1536,1536]{1,0:T(8,128)(2,1)} %bitcast.11, bf16[1536,1536]{1,0:T(8,128)(2,1)} %bitcast.12, bf16[1,3,4,96]{3,2,1,0:T(4,128)(2,1)} %bqkv_hbm.1, ...), custom_call_target="tpu_custom_call" | custom-call | tf_op jit(solution)/shard_map/stage_pipeline/pallas_call | solution.py:702
  538.8 12.2 %result_copy.1 = bf16[48,128,1536]{2,1,0:T(8,128)(2,1)} custom-call(bf16[48,128,1536]{2,1,0:T(8,128)(2,1)} %stage_pipeline.1.src), custom_call_target="tpu_custom_call" | custom-call | tf_op jit(solution)/shard_map/result_copy/pallas_call | solution.py:739

commit v8 on v7

--- a/solution.py
+++ b/solution.py
@@ -18,7 +18,7 @@
 LAGGED_STAGES = 2
 LAG_PLACES = (1, 1)
 COPY_PLACES = (0, 0)
-RELAY_UNITS = (0, 0, 4, 10)
+RELAY_UNITS = (0, 0, 5, 10)
 EAGER_UNITS = (0, 0, 3, 12)
 TURN_ROWS = 128
 COPY_ROWS = 1

time: 552 us -> 552 us (level)
  no operation moved by 1% of the time
where the time goes in v8:
time: 552 us; the launch traced here: 551 us
  Pallas kernels  551 us (100%)
    pallas_call x1, Pallas kernels, local_run(): pl.pallas_call(functools.partial(_pipeline_kernel, stages, head_dim), out...  539 us
    pallas_call x1, Pallas kernels, local_run(): pl.pallas_call(_copy_kernel, out_shape=jax.ShapeDtypeStruct((total, seq,...  12.2 us

profile of v8, /device:TPU:103, one launch (start us, length us, event | category | flops | bytes accessed | tf_op | source)
XLA Modules:
  0.0 551.0 jit_solution(2169477111760099658)
XLA Ops:
  0.0 538.8 %stage_pipeline.1.src = bf16[48,128,1536]{2,1,0:T(8,128)(2,1)} custom-call(bf16[48,128,1536]{2,1,0:T(8,128)(2,1)} %bitcast.10, bf16[1152,1536]{1,0:T(8,128)(2,1)} %bitcast.13, bf16[384,1536]{1,0:T(8,128)(2,1)} %bitcast.14, bf16[1536,1536]{1,0:T(8,128)(2,1)} %bitcast.11, bf16[1536,1536]{1,0:T(8,128)(2,1)} %bitcast.12, bf16[1,3,4,96]{3,2,1,0:T(4,128)(2,1)} %bqkv_hbm.1, ...), custom_call_target="tpu_custom_call" | custom-call | tf_op jit(solution)/shard_map/stage_pipeline/pallas_call | solution.py:702
  538.8 12.2 %result_copy.1 = bf16[48,128,1536]{2,1,0:T(8,128)(2,1)} custom-call(bf16[48,128,1536]{2,1,0:T(8,128)(2,1)} %stage_pipeline.1.src), custom_call_target="tpu_custom_call" | custom-call | tf_op jit(solution)/shard_map/result_copy/pallas_call | solution.py:739
